TPU v7x, 32 devices: a whole 2x2x4 slice. The times are simulated.
32 devices in a mesh: limb: 4 (over z), coef: 8 (over y, x, core).
Axes of the slice: x: 2, y: 2, z: 4, core: 2. Of those that a mesh axis runs over, the one named last changes fastest.
Arguments:
- cipher_zero: float32 [24, 32, 65536], P(None, 'limb', 'coef'), may hold values from -6 to 6
- cipher_one: float32 [24, 32, 65536], P(None, 'limb', 'coef'), may hold values from -6 to 6
- key_main: bfloat16 [24, 2, 2, 32, 65536], P(None, None, None, 'limb', 'coef'), may hold values from -5 to 5
- key_special: bfloat16 [24, 2, 2, 16, 65536], P(None, None, None, 'limb', 'coef'), may hold values from -5 to 5
- lift_main: float32 [32, 32], replicated, may hold values from -1.5 to 1.5
- lift_special: float32 [32, 16], replicated, may hold values from -1.5 to 1.5
- lower_table: float32 [16, 32], replicated, may hold values from -1.5 to 1.5
- inverse_scale: float32 [32], P('limb'), may hold values from 0.5 to 1.5
- inverse_main: float32 [32, 256, 256], P('limb', 'coef'), may hold values from 0.5 to 1.5
- inverse_special: float32 [16, 256, 256], P('limb', 'coef'), may hold values from 0.5 to 1.5
- forward_main: float32 [32, 256, 256], P('limb', 'coef'), may hold values from 0.5 to 1.5
- forward_special: float32 [16, 256, 256], P('limb', 'coef'), may hold values from 0.5 to 1.5
- inverse_rows: float32 [256, 256], replicated, may hold values from -0.375 to 0.375
- inverse_columns: float32 [256, 256], replicated, may hold values from -0.375 to 0.375
- forward_rows: float32 [256, 256], replicated, may hold values from -0.375 to 0.375
- forward_columns: float32 [256, 256], replicated, may hold values from -0.375 to 0.375
Outputs:
- switched_zero: float32 [24, 32, 65536], P(None, 'limb', 'coef')
- switched_one: float32 [24, 32, 65536], P(None, 'limb', 'coef')
All inputs are finite; a program needn't handle non-finite values.
Results may differ from a plain program's by a relative error of at most 0.0003.
Values sent between devices are 32-bit elements; how exact they have to be, the bound alone decides.
No kernel may reach another device: no remote copies, remote signals or barrier semaphores. Data moves between devices by JAX's collectives and lax.ppermute only.
A program may use at most 192 MiB of HBM per device.

v0:
```python
import jax
import jax.numpy as jnp
from jax import lax
from jax.sharding import PartitionSpec as P

K = 16
ROWS = 256
COLS = 256


HIGHEST = lax.Precision.HIGHEST


def columns_section(values, twiddle, inverse_columns):
    partial_value = (
        jnp.einsum("...rc,ck->...rk", values, inverse_columns, precision=HIGHEST) * twiddle
    )
    flattened = partial_value.reshape((-1,) + partial_value.shape[-2:])
    return lax.all_to_all(flattened, "coef", split_axis=2, concat_axis=1, tiled=True)


def to_coefficients(values, twiddle, inverse_rows, inverse_columns):
    leading = values.shape[:-2]
    arrived = columns_section(values, twiddle, inverse_columns)
    output = jnp.einsum("brk,rj->bkj", arrived, inverse_rows, precision=HIGHEST)
    return output.reshape(leading + output.shape[-2:])


def to_values(coeffs, twiddle, forward_rows, forward_columns):
    leading = coeffs.shape[:-2]
    partial_value = jnp.einsum("...cr,rk->...ck", coeffs, forward_rows, precision=HIGHEST) * twiddle
    flattened = partial_value.reshape((-1,) + partial_value.shape[-2:])
    arrived = lax.all_to_all(flattened, "coef", split_axis=2, concat_axis=1, tiled=True)
    output = jnp.einsum("bck,cm->bkm", arrived, forward_columns, precision=HIGHEST)
    return output.reshape(leading + output.shape[-2:])


def on_device(
    cipher_zero,
    cipher_one,
    key_main,
    key_special,
    lift_main,
    lift_special,
    lower_table,
    inverse_scale,
    inverse_main,
    inverse_special,
    forward_main,
    forward_special,
    inverse_rows,
    inverse_columns,
    forward_rows,
    forward_columns,
):
    ciphers, local_main, positions = cipher_one.shape
    local_special = key_special.shape[3]
    digits = key_main.shape[1]
    rows_here = inverse_main.shape[1]
    cols_here = forward_main.shape[1]
    total_main = lift_main.shape[0]
    limb_index = lax.axis_index("limb")
    owner = (jnp.arange(total_main) // K)[None, :] == jnp.arange(digits)[:, None]
    digit_mask = owner.astype(lift_main.dtype)
    masked_main = digit_mask[:, :, None] * lift_main[None]
    masked_special = digit_mask[:, :, None] * lift_special[None]
    twiddle_both = jnp.concatenate([forward_main, forward_special], axis=0)
    shaped = cipher_one.reshape(ciphers, local_main, rows_here, COLS)
    coeffs = to_coefficients(shaped, inverse_main, inverse_rows, inverse_columns).reshape(
        ciphers, local_main, positions
    )
    own_main = lax.dynamic_slice_in_dim(masked_main, limb_index * local_main, local_main, 2)
    own_special = lax.dynamic_slice_in_dim(
        masked_special, limb_index * local_special, local_special, 2
    )
    portion = lax.all_gather(coeffs, "limb", axis=1, tiled=True)
    lifted_main = jnp.einsum("bsn,dst->bdtn", portion, own_main, precision=HIGHEST)
    lifted_sp = jnp.einsum("bsn,dst->bdtn", portion, own_special, precision=HIGHEST)
    joined = jnp.concatenate([lifted_main, lifted_sp], axis=2)
    joined = joined.reshape(ciphers, digits, local_main + local_special, cols_here, ROWS)
    values_all = to_values(joined, twiddle_both, forward_rows, forward_columns)
    values_all = values_all.reshape(ciphers, digits, local_main + local_special, positions)
    values_main = values_all[:, :, :local_main]
    values_sp = values_all[:, :, local_main:]
    summed_main = jnp.sum(values_main[:, :, None] * key_main.astype(jnp.float32), axis=1)
    summed_sp = jnp.sum(values_sp[:, :, None] * key_special.astype(jnp.float32), axis=1)
    shaped_sp = summed_sp.reshape(ciphers, 2, local_special, rows_here, COLS)
    special = to_coefficients(shaped_sp, inverse_special, inverse_rows, inverse_columns)
    special = special.reshape(ciphers, 2, local_special, positions)
    own_lower = lax.dynamic_slice_in_dim(lower_table, limb_index * local_main, local_main, 1)
    lowered = jnp.einsum(
        "bsjn,jt->bstn",
        lax.all_gather(special, "limb", axis=2, tiled=True),
        own_lower,
        precision=HIGHEST,
    )
    lowered = to_values(
        lowered.reshape(ciphers, 2, local_main, cols_here, ROWS),
        forward_main,
        forward_rows,
        forward_columns,
    )
    lowered = lowered.reshape(ciphers, 2, local_main, positions)
    result = inverse_scale[:, None] * (summed_main - lowered)
    return (cipher_zero + result[:, 0], result[:, 1])


def solution(mesh):
    placed = (
        P(None, "limb", "coef"),
        P(None, "limb", "coef"),
        P(None, None, None, "limb", "coef"),
        P(None, None, None, "limb", "coef"),
        P(),
        P(),
        P(),
        P("limb"),
        P("limb", "coef", None),
        P("limb", "coef", None),
        P("limb", "coef", None),
        P("limb", "coef", None),
        P(),
        P(),
        P(),
        P(),
    )
    return jax.shard_map(
        on_device,
        mesh=mesh,
        in_specs=placed,
        out_specs=(P(None, "limb", "coef"), P(None, "limb", "coef")),
        check_vma=False,
    )
```

profile of v0, /device:TPU:0, one launch (start us, length us, event | category | flops | bytes accessed | tf_op | source)
XLA Modules:
  0.0 1902.5 jit_solution(8218457899947715766)
XLA Ops:
  7.2 10.8 broadcast_multiply_fusion.3
  18.0 9.6 copy.48
  27.6 99.7 %all_to_all.72 = f32[192,32,256]{0,1,2:T(8,128)S(1)} all-to-all(f32[192,32,256]{0,1,2:T(8,128)} %copy.48), channel_id=1, replica_groups=mesh['limb'=4,'coef'=8] {'coef'}, dimensions={2} | all-to-all | bytes 12582912 | tf_op jit(solution)/shard_map/all_to_all | solution.py:19
  127.3 8.0 copy.50
  135.2 9.7 copy.51
  145.0 8.8 fusion.35
  153.8 7.2 reshape_reshape.12
  161.0 0.2 all-gather.5.cloned.1.call-start
  161.3 0.7 constant_dynamic-slice_fusion
  162.1 0.6 compare_convert_fusion
  162.7 423.1 %all-gather.3.cloned.1.call-done = f32[24,32,8192]{2,1,0:T(8,128)} async-done(((f32[24,8,8192]{2,1,0:T(8,128)}), f32[24,32,8192]{2,1,0:T(8,128)}) %all-gather.3.cloned.1.call-update) | async-done | bytes 25165840 | tf_op jit(solution)/shard_map/all_gather | solution.py:76
  585.8 16.9 fusion.13
  602.7 15.7 fusion.10
  618.5 14.2 pad_maximum_fusion
  632.7 21.5 %reshape.87 = f32[24,2,12,32,256]{4,3,2,0,1:T(8,128)} reshape(f32[24,2,12,8192]{3,2,0,1:T(8,128)} %pad_maximum_fusion) | data formatting | bytes 37748736 | tf_op jit(solution)/shard_map/reshape | solution.py:80
  654.2 20.6 %broadcast_multiply_fusion = f32[24,2,12,32,256]{4,3,2,1,0:T(8,128)} fusion(f32[12,32,256]{2,1,0:T(8,128)S(1)} %pad_maximum_fusion.1, f32[24,2,12,32,256]{4,3,2,0,1:T(8,128)} %reshape.87, f32[256,256]{1,0:T(8,128)S(1)} %copy-done), kind=kOutput, calls=%fused_computation.16 | convolution fusion | flops 14500233216 | bytes 38404096 | tf_op jit(solution)/shard_map/...cr,rk->...ck/dot_general | solution.py:31
  674.8 23.4 %copy.54 = f32[576,32,256]{0,1,2:T(8,128)} copy(f32[576,32,256]{2,1,0:T(8,128)} %bitcast.95) | data formatting | bytes 37748736 | tf_op jit(solution)/shard_map/reshape | solution.py:32
  698.2 233.5 %all_to_all.73 = f32[576,32,256]{0,1,2:T(8,128)S(1)} all-to-all(f32[576,32,256]{0,1,2:T(8,128)} %copy.54), channel_id=1, replica_groups=mesh['limb'=4,'coef'=8] {'coef'}, dimensions={2} | all-to-all | bytes 37748736 | tf_op jit(solution)/shard_map/all_to_all | solution.py:33
  931.8 14.1 copy.56
  945.9 21.5 %copy.57 = f32[576,256,32]{1,2,0:T(8,128)} copy(f32[576,256,32]{0,2,1:T(8,128)} %bitcast.97) | data formatting | bytes 37748736 | tf_op jit(solution)/shard_map/all_to_all | solution.py:33
  967.4 20.2 %fusion.31 = f32[576,32,256]{2,1,0:T(8,128)} fusion(f32[576,256,32]{1,2,0:T(8,128)} %copy.57, f32[256,256]{1,0:T(8,128)S(1)} %copy-done.2), kind=kOutput, calls=%fused_computation.32 | convolution fusion | flops 14495514624 | bytes 38010880 | tf_op jit(solution)/shard_map/bck,cm->bkm/dot_general | solution.py:34
  987.6 20.6 %reshape_reshape.13 = f32[24,2,12,8192]{3,2,1,0:T(8,128)} reshape(f32[576,32,256]{2,1,0:T(8,128)} %fusion.31) | data formatting | bytes 37748736 | tf_op jit(solution)/shard_map/reshape;reshape | solution.py:82
  1008.1 5.5 slice.17
  1013.7 11.3 multiply_reduce_fusion.1
  1025.0 8.5 reshape.74
  1033.5 9.1 broadcast_multiply_fusion.2
  1042.6 9.6 copy.59
  1052.2 97.8 %all_to_all.74 = f32[192,32,256]{0,1,2:T(8,128)S(1)} all-to-all(f32[192,32,256]{0,1,2:T(8,128)} %copy.59), channel_id=1, replica_groups=mesh['limb'=4,'coef'=8] {'coef'}, dimensions={2} | all-to-all | bytes 12582912 | tf_op jit(solution)/shard_map/all_to_all | solution.py:19
  1149.9 8.0 copy.61
  1157.9 9.7 copy.62
  1167.6 8.8 fusion.33
  1176.5 8.6 reshape_reshape.14
  1185.1 9.1 copy.63
  1194.3 421.7 %all-gather.5.cloned.1.call-done = f32[24,2,16,8192]{3,0,1,2:T(8,128)} async-done(((f32[24,2,4,8192]{3,0,1,2:T(8,128)}), f32[24,2,16,8192]{3,0,1,2:T(8,128)}) %all-gather.5.cloned.1.call-update) | async-done | bytes 25165840 | tf_op jit(solution)/shard_map/all_gather | solution.py:93
  1615.9 34.7 %fusion.4 = f32[8,24,2,8192]{3,0,2,1:T(8,128)S(1)} fusion(f32[24,2,16,8192]{3,0,1,2:T(8,128)} %all-gather.5.cloned.1.call-done, f32[16,32]{1,0:T(8,128)S(1)} %copy-done.12, s32[]{:T(128)S(6)} %select_n.19), kind=kOutput, calls=%fused_computation.5 | convolution fusion | flops 603979776 | bytes 37750788 | tf_op jit(solution)/shard_map/bsjn,jt->bstn/dot_general | solution.py:91
  1650.7 13.7 broadcast_multiply_fusion.1
  1664.4 12.9 copy.66
  1677.2 5.4 all-to-all-start.3
  1682.6 10.4 slice.16
  1693.1 15.5 multiply_reduce_fusion
  1708.6 113.0 %all-to-all-done.3 = f32[384,32,256]{0,1,2:T(8,128)} async-done(((f32[384,32,256]{0,1,2:T(8,128)}), f32[384,32,256]{0,1,2:T(8,128)}, u32[]{:S(2)}, u32[]{:S(2)}) %all-to-all-start.3) | async-done | bytes 12582944 | tf_op jit(solution)/shard_map/all_to_all | solution.py:33
  1821.6 16.1 copy.68
  1837.8 12.9 copy.77
  1850.7 14.9 fusion.29
  1865.6 14.0 reshape_reshape.15
  1879.6 9.3 subtract_multiply_fusion
  1888.9 3.1 slice_bitcast_fusion
  1892.1 3.3 fusion.18
  (40 shorter events, 0.2 us)
Async XLA Ops:
  7.2 647.0 %copy-start = (f32[256,256]{1,0:T(8,128)S(1)}, f32[256,256]{1,0:T(8,128)}, u32[]{:S(2)}) copy-start(f32[256,256]{1,0:T(8,128)} %param.30) | copy-start | bytes 786436
  7.2 578.6 %all-gather.3.cloned.1.call-start = ((), (), s32[]{:S(2)}) async-start(), calls=%async_computation.4 | async-start | bytes 31457280 | tf_op jit(solution)/shard_map/all_gather | solution.py:76
  127.3 17.7 copy-start.7
  153.8 7.5 copy-start.11
  153.8 8.2 copy-start.4
  153.8 8.2 copy-start.10
  161.0 1454.9 %all-gather.5.cloned.1.call-start = ((), (), s32[]{:S(2)}) async-start(), calls=%async_computation.5 | async-start | bytes 31457280 | tf_op jit(solution)/shard_map/all_gather | solution.py:93
  585.8 17.0 copy-start.1
  945.9 21.5 %copy-start.2 = (f32[256,256]{1,0:T(8,128)S(1)}, f32[256,256]{1,0:T(8,128)}, u32[]{:S(2)}) copy-start(f32[256,256]{1,0:T(8,128)} %param.31) | copy-start | bytes 786436
  1013.7 19.9 %copy-start.9 = (f32[4,32,256]{2,1,0:T(8,128)S(1)}, f32[4,32,256]{2,1,0:T(8,128)}, u32[]{:S(2)}) copy-start(f32[4,32,256]{2,1,0:T(8,128)} %param.25) | copy-start | bytes 393220
  1025.0 8.5 copy-start.6
  1149.9 17.7 copy-start.8
  1185.1 430.8 %copy-start.12 = (f32[16,32]{1,0:T(8,128)S(1)}, f32[16,32]{1,0:T(8,128)}, u32[]{:S(2)}) copy-start(f32[16,32]{1,0:T(8,128)} %param.22) | copy-start | bytes 6148
  1194.2 456.4 %copy-start.5 = (f32[8,32,256]{2,1,0:T(8,128)S(1)}, f32[8,32,256]{2,1,0:T(8,128)}, u32[]{:S(2)}) copy-start(f32[8,32,256]{2,1,0:T(8,128)} %param.26) | copy-start | bytes 786436
  1677.2 144.4 %all-to-all-start.3 = ((f32[384,32,256]{0,1,2:T(8,128)}), f32[384,32,256]{0,1,2:T(8,128)}, u32[]{:S(2)}, u32[]{:S(2)}) async-start(f32[384,32,256]{0,1,2:T(8,128)} %copy.66), calls=%async_computation.3 | async-start | bytes 25165824 | tf_op jit(solution)/shard_map/all_to_all | solution.py:33
  1837.8 12.9 copy-start.3
  1865.6 14.0 copy-start.13
  1865.6 26.4 %slice-start = ((s8[6291456]{0:T(1024)(128)(4,1)}), s8[2097152]{0:T(1024)(128)(4,1)S(1)}, s32[]{:S(2)}) async-start(s8[6291456]{0:T(1024)(128)(4,1)} %bitcast.108), calls=%async_computation.6 | async-start | bytes 4194304
  1879.6 12.4 slice-start.1
Sparse Core Ops, SparseCore 0:
  161.1 424.5 all-gather.2
  1194.4 421.5 all-gather.4
where the time goes:
time: 1910 us; the launch traced here: 1900 us
  waiting for transfers between devices  958 us (50%)
  blocking collectives  431 us (23%)
  local copies, waits for them, and re-layouts  265 us (14%)
  matrix products  174 us (9%)
  other arithmetic  54.3 us (3%)
    all_gather x1, waiting for transfers between devices, on_device(): portion = lax.all_gather(coeffs, 'limb', axis=1, tiled=True)  423 us
    all_gather x1, waiting for transfers between devices, on_device(): lax.all_gather(special, 'limb', axis=2, tiled=True)  422 us
    all_to_all x1, blocking collectives, to_values(): lax.all_to_all(flattened, 'coef', split_axis=2, concat_axis=1, tiled=True)  234 us
    all_to_all x2, blocking collectives, columns_section(): lax.all_to_all(flattened, 'coef', split_axis=2, concat_axis=1, tiled=True)  197 us
    all_to_all x1, waiting for transfers between devices, to_values(): lax.all_to_all(flattened, 'coef', split_axis=2, concat_axis=1, tiled=True)  113 us
    all_to_all x4, local copies, waits for them, and re-layouts, to_values(): lax.all_to_all(flattened, 'coef', split_axis=2, concat_axis=1, tiled=True)  64.7 us
  transfers between devices with their start and end apart: 3, of which 3 were waited for; matrix products, arithmetic and copies ran while one was open for 1% of the time, Pallas kernels for 0%

commit v1 on v0

--- a/solution.py
+++ b/solution.py
@@ -1,11 +1,19 @@
+import functools
+
 import jax
 import jax.numpy as jnp
 from jax import lax
+from jax.experimental import pallas as pl
+from jax.experimental.pallas import tpu as pltpu
 from jax.sharding import PartitionSpec as P
+
 
 K = 16
 ROWS = 256
 COLS = 256
+SIZES = (2, 4, 4, 4, 4, 4, 2)
+F32 = jnp.float32
+BF16 = jnp.bfloat16
 
 
 HIGHEST = lax.Precision.HIGHEST
@@ -35,7 +43,7 @@
     return output.reshape(leading + output.shape[-2:])
 
 
-def on_device(
+def general(
     cipher_zero,
     cipher_one,
     key_main,
@@ -105,6 +113,436 @@
     return (cipher_zero + result[:, 0], result[:, 1])
 
 
+def halves(x):
+    high = lax.reduce_precision(x, 8, 7)
+    return high.astype(BF16), (x - high).astype(BF16)
+
+
+def split(x):
+    high = x.astype(BF16)
+    return high, (x - high.astype(F32)).astype(BF16)
+
+
+def mm(a, b):
+    return jnp.dot(a, b, preferred_element_type=F32)
+
+
+def mm3(a, b):
+    return mm(a[0], b[0]) + (mm(a[1], b[0]) + mm(a[0], b[1]))
+
+
+def put(scr, x, start=0):
+    half = scr.shape[2]
+    for h in range(scr.shape[0]):
+        scr[h, pl.ds(start, x.shape[0]), :] = x[:, h * half : (h + 1) * half]
+
+
+def first_kernel(x, tw, wh, wl, out, scr, *, rows, cols):
+    limbs = x.shape[1]
+    stacked = jnp.concatenate([x[0, :, r * cols : (r + 1) * cols] for r in range(rows)], axis=0)
+    put(scr, mm3(split(stacked), (wh[...], wl[...])) * tw[...])
+    half = scr.shape[2]
+    for d in range(limbs):
+        for h in range(scr.shape[0]):
+            out[d, 0, :, h * half : (h + 1) * half] = scr[h, pl.ds(d, rows, stride=limbs), :]
+
+
+def middle_kernel(x, mh, ml, out):
+    n, _, rows, cols = x.shape
+    y = mm3((mh[...], ml[...]), split(x[...].reshape(n * rows, cols)))
+    out[...] = y.reshape(n, 1, rows, cols)
+
+
+GROUP = 4
+TILE = 16
+
+
+def lift(emit, groups, coef, refs, rows):
+    def body(g, carry):
+        for row in range(0, rows, TILE):
+            sums = [None] * GROUP
+            for k, (ref, s) in enumerate(refs):
+                poly = ref[s, 0, row : row + TILE, :]
+                for j in range(GROUP):
+                    add = coef(g * GROUP + j, k) * poly
+                    sums[j] = add if sums[j] is None else sums[j] + add
+            for j in range(GROUP):
+                emit(g * GROUP + j, row, sums[j])
+        return carry
+
+    lax.fori_loop(0, groups, body, 0)
+
+
+def key_kernel(coef, polys, fw, ch, cl, ih, il, tws, km, ks, out, summed, vh, vl, wv, xs, ys):
+    both, rows, cols = fw.shape
+    digits, main = km.shape[1], km.shape[3]
+    special = ks.shape[3]
+    lanes, _, half = wv.shape
+    span = polys.shape[0] // digits
+
+    for d in range(digits):
+
+        def emit(t, row, value, d=d):
+            high, low = split(value * fw[t, row : row + TILE, :])
+            at = pl.multiple_of((d * both + t) * rows + row, TILE)
+            vh[pl.ds(at, TILE), :] = high
+            vl[pl.ds(at, TILE), :] = low
+
+        lift(
+            emit,
+            both // GROUP,
+            lambda t, k, d=d: coef[d, t, k],
+            [(polys, d * span + s) for s in range(span)],
+            rows,
+        )
+
+    put(wv, mm3((vh[...], vl[...]), (ch[...], cl[...])))
+
+    def keys(r, carry):
+        for h in range(lanes):
+            at = pl.multiple_of(r * cols + h * half, half)
+            for keyed, base, count in ((km, 0, main), (ks, main, special)):
+                values = [
+                    wv[h, pl.ds((d * both + base) * rows + r, count, stride=rows), :]
+                    for d in range(digits)
+                ]
+                for i in range(2):
+                    total = None
+                    for d in range(digits):
+                        add = values[d] * keyed[0, d, i, :, pl.ds(at, half)].astype(F32)
+                        total = add if total is None else total + add
+                    if base == 0:
+                        summed[0, i, :, pl.ds(at, half)] = total
+                    else:
+                        xs[i, r, :, h * half : (h + 1) * half] = total
+        return carry
+
+    lax.fori_loop(0, rows, keys, 0, unroll=4)
+    size = rows * special
+    y = mm3(split(xs[...].reshape(2 * size, cols)), (ih[...], il[...]))
+    for i in range(2):
+        put(ys, y[i * size : (i + 1) * size] * tws[...], i * size)
+    for i in range(2):
+        for u in range(special):
+            for h in range(lanes):
+                out[i * special + u, 0, :, h * half : (h + 1) * half] = ys[
+                    h, pl.ds(i * size + u, rows, stride=special), :
+                ]
+
+
+def end_lower_kernel(coef, *refs):
+    ins, out = refs[:-1], refs[-1]
+    u = ins[0].shape[0] // 2
+    per, rows = out.shape[0] // 2, out.shape[2]
+    for i in range(2):
+
+        def emit(t, row, value, i=i):
+            out[i * per + t, 0, row : row + TILE, :] = value
+
+        lift(
+            emit,
+            per // GROUP,
+            lambda t, k: coef[t, k],
+            [(ref, i * u + s) for ref in ins for s in range(u)],
+            rows,
+        )
+
+
+def last_kernel(coef, own, mate, cross, far, ready, fw, ch, cl, scale, summed, zero, *rest):
+    out0, out1, done, vh, vl, wv = rest[-6:]
+    done[...] = jnp.zeros(done.shape, F32)
+    per, rows, cols = fw.shape
+    u = own.shape[0] // 2
+    lanes, _, half = wv.shape
+    for i in range(2):
+
+        def emit(t, row, value, i=i):
+            value = value + ready[i * per + t, 0, row : row + TILE, :]
+            high, low = split(value * fw[t, row : row + TILE, :])
+            at = pl.multiple_of((i * per + t) * rows + row, TILE)
+            vh[pl.ds(at, TILE), :] = high
+            vl[pl.ds(at, TILE), :] = low
+
+        lift(
+            emit,
+            per // GROUP,
+            lambda t, k: coef[t, k],
+            [(ref, i * u + s) for ref in (own, mate, cross, far) for s in range(u)],
+            rows,
+        )
+    put(wv, mm3((vh[...], vl[...]), (ch[...], cl[...])))
+    factor = jnp.broadcast_to(scale[...], (per, half))
+
+    def finish(r, carry):
+        for h in range(lanes):
+            at = pl.multiple_of(r * cols + h * half, half)
+            for i, out in enumerate((out0, out1)):
+                low = wv[h, pl.ds(i * per * rows + r, per, stride=rows), :]
+                value = factor * (summed[0, i, :, pl.ds(at, half)] - low)
+                if i == 0:
+                    value = zero[0, :, pl.ds(at, half)] + value
+                out[0, :, pl.ds(at, half)] = value
+        return carry
+
+    lax.fori_loop(0, rows, finish, 0, unroll=4)
+
+
+def fast(
+    cipher_zero,
+    cipher_one,
+    key_main,
+    key_special,
+    lift_main,
+    lift_special,
+    lower_table,
+    inverse_scale,
+    inverse_main,
+    inverse_special,
+    forward_main,
+    forward_special,
+    inverse_rows,
+    inverse_columns,
+    forward_rows,
+    forward_columns,
+):
+    ciphers, main, positions = cipher_one.shape
+    digits = key_main.shape[1]
+    special = key_special.shape[3]
+    rows, cols = inverse_main.shape[1:]
+    n = main
+    half = min(cols, 128)
+    lanes = cols // half
+    both = main + special
+    z = lax.axis_index("limb")
+    inner = jnp.logical_or(z == 1, z == 2).astype(F32)
+
+    merged = halves(jnp.einsum("rj,jk->kr", inverse_rows, forward_rows, precision=HIGHEST))
+    ic = halves(inverse_columns)
+    fc = halves(forward_columns)
+    tw_in = inverse_main.transpose(1, 0, 2).reshape(rows * main, cols)
+    tw_sp = inverse_special.transpose(1, 0, 2).reshape(rows * special, cols)
+    fw = jnp.concatenate([forward_main, forward_special], axis=0)
+    fw = fw.transpose(2, 0, 1).reshape(n, rows * both * rows // cols, cols)
+    fw = lax.all_to_all(fw, "coef", split_axis=0, concat_axis=0)
+    fw = fw.reshape(n, rows, both, rows).transpose(2, 1, 0, 3).reshape(both, rows, cols)
+    fw_main = fw[:main]
+
+    def columns(full, target, count):
+        return lax.dynamic_slice_in_dim(full, target * count, count, 1).T
+
+    def lower_from(source, target):
+        full = lax.dynamic_slice_in_dim(lower_table, source * special, special, 0)
+        return columns(full, target, main)
+
+    coef_lift = jnp.concatenate(
+        [columns(lift_main, z, main), columns(lift_special, z, special)], axis=0
+    )
+    coef_lift = coef_lift.reshape(both, digits, K).transpose(1, 0, 2)
+    mate_z = z ^ 1
+    cross_z = 3 - z
+    far_z = cross_z ^ 1
+    coef_low = jnp.concatenate(
+        [lower_from(z, z)]
+        + [inner * lower_from(source, z) for source in (mate_z, cross_z, far_z)],
+        axis=1,
+    )
+    coef_low_end = jnp.concatenate(
+        [lower_from(source, mate_z) for source in (z, cross_z, far_z)], axis=1
+    )
+    scale = inverse_scale[:, None]
+
+    smem = pl.BlockSpec(memory_space=pltpu.SMEM)
+
+    def whole(x):
+        return pl.BlockSpec(x.shape, lambda c: (0,) * x.ndim)
+
+    def polys(count):
+        return pl.BlockSpec((count, 1, rows, cols), lambda c: (0, c, 0, 0))
+
+    def stacked(count, size):
+        return jax.ShapeDtypeStruct((count, size, rows, cols), F32)
+
+    def call(kernel, size, in_specs, out_specs, out_shape, scratch, flops, **kw):
+        def after(_, *refs):
+            kernel(*refs)
+
+        return pl.pallas_call(
+            after,
+            grid=(size,),
+            in_specs=[pl.BlockSpec(memory_space=pl.ANY)] + in_specs,
+            out_specs=out_specs,
+            scratch_shapes=scratch,
+            out_shape=out_shape,
+            compiler_params=pltpu.CompilerParams(
+                dimension_semantics=("arbitrary",), vmem_limit_bytes=40 * 1024 * 1024
+            ),
+            cost_estimate=pl.CostEstimate(
+                flops=int(flops * size), transcendentals=0, bytes_accessed=0
+            ),
+            **kw,
+        )
+
+    def first(start, size):
+        return call(
+            functools.partial(first_kernel, rows=rows, cols=cols),
+            size,
+            [
+                pl.BlockSpec((1, main, positions), lambda c: (start + c, 0, 0)),
+                whole(tw_in),
+                whole(ic[0]),
+                whole(ic[1]),
+            ],
+            polys(n),
+            stacked(n, size),
+            [pltpu.VMEM((lanes, rows * main, half), F32)],
+            1e6,
+        )
+
+    def middle(size):
+        return call(
+            middle_kernel,
+            size,
+            [polys(n), whole(merged[0]), whole(merged[1])],
+            polys(n),
+            stacked(n, size),
+            [],
+            1e6,
+        )
+
+    def keyed(start, size):
+        return call(
+            key_kernel,
+            size,
+            [smem, polys(digits * K)]
+            + [whole(x) for x in (fw, *fc, *ic, tw_sp)]
+            + [
+                pl.BlockSpec((1, digits, 2, main, positions), lambda c: (start + c, 0, 0, 0, 0)),
+                pl.BlockSpec((1, digits, 2, special, positions), lambda c: (start + c, 0, 0, 0, 0)),
+            ],
+            [polys(n), pl.BlockSpec((1, 2, main, positions), lambda c: (c, 0, 0, 0))],
+            [stacked(n, size), jax.ShapeDtypeStruct((size, 2, main, positions), F32)],
+            [
+                pltpu.VMEM((digits * both * rows, cols), BF16),
+                pltpu.VMEM((digits * both * rows, cols), BF16),
+                pltpu.VMEM((lanes, digits * both * rows, half), F32),
+                pltpu.VMEM((2, rows, special, cols), F32),
+                pltpu.VMEM((lanes, 2 * rows * special, half), F32),
+            ],
+            4e6,
+        )
+
+    def end_lower(size):
+        return call(
+            end_lower_kernel,
+            size,
+            [smem] + [polys(n)] * 3,
+            polys(2 * main),
+            stacked(2 * main, size),
+            [],
+            1e6,
+        )
+
+    def last(outs, start, size):
+        block = pl.BlockSpec((1, main, positions), lambda c: (start + c, 0, 0))
+        kw = {} if outs is None else {"input_output_aliases": {13: 0, 14: 1}}
+        return call(
+            last_kernel,
+            size,
+            [smem]
+            + [polys(n)] * 4
+            + [polys(2 * main)]
+            + [whole(x) for x in (fw_main, *fc, scale)]
+            + [pl.BlockSpec((1, 2, main, positions), lambda c: (c, 0, 0, 0)), block]
+            + ([] if outs is None else [pl.BlockSpec(memory_space=pl.ANY)] * 2),
+            [block, block, pl.BlockSpec((8, half), lambda c: (0, 0))],
+            [jax.ShapeDtypeStruct(cipher_zero.shape, F32)] * 2
+            + [jax.ShapeDtypeStruct((8, half), F32)],
+            [
+                pltpu.VMEM((2 * main * rows, cols), BF16),
+                pltpu.VMEM((2 * main * rows, cols), BF16),
+                pltpu.VMEM((lanes, 2 * main * rows, half), F32),
+            ],
+            3e6,
+            **kw,
+        )
+
+    def exchange(x):
+        return lax.all_to_all(x, "coef", split_axis=0, concat_axis=0, tiled=True)
+
+    def inward(x):
+        return lax.ppermute(x, "limb", [(0, 1), (3, 2)])
+
+    def across(x):
+        return lax.ppermute(x, "limb", [(1, 2), (2, 1)])
+
+    def outward(x):
+        return lax.ppermute(x, "limb", [(1, 0), (2, 3)])
+
+    chunks = []
+    at = 0
+    for size in SIZES if sum(SIZES) == ciphers else [1] * ciphers:
+        chunks.append((at, size))
+        at += size
+
+    state = [{} for _ in chunks]
+    token = tw_in
+    outs = None
+    for c, stage in schedule(len(chunks)):
+        start, size = chunks[c]
+        st = state[c]
+
+        if stage == "A":
+            token = y = first(start, size)(token, cipher_one, tw_in, *ic)
+        elif stage in "BE":
+            token = y = middle(size)(token, st["x"], *merged)
+        elif stage == "D":
+            y, st["summed"] = keyed(start, size)(
+                token, coef_lift, st["x"], fw, *fc, *ic, tw_sp, key_main, key_special
+            )
+            token = y
+        elif stage == "F":
+            own, mate, cross, far = st["x"]
+            token = y = end_lower(size)(token, coef_low_end, own, cross, far)
+        else:
+            extra = () if outs is None else outs
+            *outs, token = last(outs, start, size)(
+                token,
+                coef_low,
+                *st["x"],
+                st["ready"],
+                fw_main,
+                *fc,
+                scale,
+                st["summed"],
+                cipher_zero,
+                *extra,
+            )
+        if stage in "ABDE":
+            y = exchange(y)
+        if stage == "B":
+            y = lax.all_gather(y, "limb", axis=0, tiled=True)
+        if stage == "E":
+            own = y
+            mate = inward(own)
+            cross = across(own)
+            far = across(mate)
+            y = (own, mate, cross, far)
+        if stage == "F":
+            st["ready"] = outward(y)
+        else:
+            st["x"] = y
+    return tuple(outs)
+
+
+def schedule(n):
+    order = [(0, "A"), (0, "B"), (1, "A"), (1, "B")]
+    for s in range(n - 1):
+        order += [(s, "D"), (s + 2, "A"), (s, "E"), (s - 1, "F"), (s + 2, "B"), (s - 2, "G")]
+    s = n - 1
+    order += [(s, "D"), (s - 1, "F"), (s, "E"), (s - 2, "G"), (s - 1, "G"), (s, "F"), (s, "G")]
+    return [(c, stage) for c, stage in order if 0 <= c < n]
+
+
 def solution(mesh):
     placed = (
         P(None, "limb", "coef"),
@@ -124,6 +562,26 @@
         P(),
         P(),
     )
+    limb = mesh.shape["limb"]
+    coef = mesh.shape["coef"]
+
+    def on_device(*args):
+        main = args[1].shape[1]
+        special = args[3].shape[3]
+        digits = args[2].shape[1]
+        suits = (
+            limb == 4
+            and digits == 2
+            and main == 8
+            and special == 4
+            and coef == main
+            and 2 * K == limb * main
+            and args[8].shape[1] * coef == ROWS == COLS
+        )
+        if suits:
+            return fast(*args)
+        return general(*args)
+
     return jax.shard_map(
         on_device,
         mesh=mesh,

time: 1910 us -> 1170 us (0.61)
  waiting for transfers between devices: 958 us -> 350 us
  starting transfers between devices: 5.67 us -> 283 us
  blocking collectives: 431 us -> 206 us
  Pallas kernels: 0 us -> 190 us
  matrix products: 174 us -> 0.6 us
  local copies, waits for them, and re-layouts: 265 us -> 114 us
  other arithmetic: 54.3 us -> 1.33 us
    all_gather x2 -> x7, waiting for transfers between devices: 845 us -> 0.05 us  [fast(): y = lax.all_gather(y, 'limb', axis=0, tiled=True)]
    ppermute x0 -> x28, waiting for transfers between devices: none -> 259 us  [the longest x7 176 us: outward(): return lax.ppermute(x, 'limb', [(1, 0), (2, 3)])]
    all_to_all x3 -> x12, blocking collectives: 431 us -> 206 us  [exchange(): return lax.all_to_all(x, 'coef', split_axis=0, concat_axis=0, tiled=True)]
    ppermute x0 -> x28, starting transfers between devices: none -> 214 us  [the longest x7 186 us: inward(): return lax.ppermute(x, 'limb', [(0, 1), (3, 2)])]
    pallas_call x0 -> x42, Pallas kernels: none -> 190 us  [the longest x7 76.2 us: fast(): keyed(start, size)]
    dot_general x11 -> x1, matrix products: 174 us -> 0.6 us  [fast(): jnp.einsum('rj,jk->kr', inverse_rows, forward_rows, precision=HIGHEST)]
    all_to_all x8 -> x0, local copies, waits for them, and re-layouts: 100 us -> none  [the longest x4 64.7 us: to_values(): lax.all_to_all(flattened, 'coef', split_axis=2, concat_axis=1, tiled=True)]
    unnamed x33 -> x177, local copies, waits for them, and re-layouts: 0.14 us -> 94.1 us
  transfers between devices with their start and end apart: 3 -> 52, of which waited for: 3 -> 21; matrix products, arithmetic and copies ran while one was open for 1% -> 2% of each run, Pallas kernels for 0% -> 16%
where the time goes in v1:
time: 1170 us; the launch traced here: 1160 us
  waiting for transfers between devices  350 us (30%)
  starting transfers between devices  283 us (24%)
  blocking collectives  206 us (18%)
  Pallas kernels  190 us (16%)
  local copies, waits for them, and re-layouts  114 us (10%)
  between operations  15.5 us (1%)
    all_to_all x12, blocking collectives, exchange(): return lax.all_to_all(x, 'coef', split_axis=0, concat_axis=0, tiled=True)  206 us
    ppermute x7, starting transfers between devices, inward(): return lax.ppermute(x, 'limb', [(0, 1), (3, 2)])  186 us
    ppermute x7, waiting for transfers between devices, outward(): return lax.ppermute(x, 'limb', [(1, 0), (2, 3)])  176 us
    unnamed x177, local copies, waits for them, and re-layouts  94.1 us
    all_to_all x16, waiting for transfers between devices, exchange(): return lax.all_to_all(x, 'coef', split_axis=0, concat_axis=0, tiled=True)  83.1 us
    ppermute x7, waiting for transfers between devices, inward(): return lax.ppermute(x, 'limb', [(0, 1), (3, 2)])  83 us
    pallas_call x7, Pallas kernels, fast(): keyed(start, size)  76.2 us
    all_to_all x16, starting transfers between devices, exchange(): return lax.all_to_all(x, 'coef', split_axis=0, concat_axis=0, tiled=True)  64.7 us
  transfers between devices with their start and end apart: 52, of which 21 were waited for; matrix products, arithmetic and copies ran while one was open for 2% of the time, Pallas kernels for 16%

profile of v1, /device:TPU:0, one launch (start us, length us, event | category | flops | bytes accessed | tf_op | source)
XLA Modules:
  0.0 1159.7 jit_solution(5885302851337230167)
XLA Ops:
  19.3 9.0 all-to-all-done.refs_0_
  29.0 12.8 %all_to_all.145 = f32[8,2,32,256]{3,2,1,0:T(8,128)} all-to-all(f32[8,2,32,256]{3,2,1,0:T(8,128)S(1)} %shard_map.168._), channel_id=1, replica_groups=mesh['limb'=4,'coef'=8] {'coef'}, dimensions={0} | all-to-all | bytes 1048576 | tf_op jit(solution)/shard_map/all_to_all | solution.py:470
  45.9 17.9 %all_to_all.146.refs_0_ = f32[8,4,32,256]{3,2,1,0:T(8,128)S(1)} all-to-all(f32[8,4,32,256]{3,2,1,0:T(8,128)S(1)} %shard_map.169._), channel_id=1, replica_groups=mesh['limb'=4,'coef'=8] {'coef'}, dimensions={0} | all-to-all | bytes 2097152 | tf_op jit(solution)/shard_map/all_to_all | solution.py:470
  65.0 18.4 %all_to_all.147 = f32[8,4,32,256]{3,2,1,0:T(8,128)} all-to-all(f32[8,4,32,256]{3,2,1,0:T(8,128)S(1)} %shard_map.170._), channel_id=1, replica_groups=mesh['limb'=4,'coef'=8] {'coef'}, dimensions={0} | all-to-all | bytes 2097152 | tf_op jit(solution)/shard_map/all_to_all | solution.py:470
  93.6 7.0 all-to-all-done.3
  112.5 6.6 shard_map.171
  140.9 12.8 %all-to-all-done.5.refs_0_ = f32[8,4,32,256]{3,2,1,0:T(8,128)S(1)} async-done(((f32[8,4,32,256]{3,2,1,0:T(8,128)}), f32[8,4,32,256]{3,2,1,0:T(8,128)S(1)}, u32[]{:S(2)}, u32[]{:S(2)}) %all-to-all-start.5) | async-done | bytes 1048608 | tf_op jit(solution)/shard_map/all_to_all | solution.py:470
  158.2 18.5 %all_to_all.148 = f32[8,4,32,256]{3,2,1,0:T(8,128)} all-to-all(f32[8,4,32,256]{3,2,1,0:T(8,128)S(1)} %shard_map.174._), channel_id=1, replica_groups=mesh['limb'=4,'coef'=8] {'coef'}, dimensions={0} | all-to-all | bytes 2097152 | tf_op jit(solution)/shard_map/all_to_all | solution.py:470
  183.2 12.4 %shard_map.175 = (f32[8,4,32,256]{3,2,1,0:T(8,128)S(1)}, f32[4,2,8,8192]{3,2,1,0:T(8,128)S(1)}) custom-call(f32[8,4,32,256]{3,2,1,0:T(8,128)S(1)} %shard_map.174._, f32[2,12,16]{2,1,0:T(8,128)S(1)} %bitcast.42, f32[32,4,32,256]{3,2,1,0:T(8,128)S(1)} %copy-done.52, f32[12,32,256]{2,1,0:T(8,128)S(1)} %reshape.27.refs_2_, ...), custom_call_target="tpu_custom_call" | custom-call | flops 16000000 | tf_op jit(solution)/shard_map/pallas_call | solution.py:499
  223.1 6.2 collective-permute-done.1.refs_2_
  239.8 18.7 %all_to_all.149 = f32[8,4,32,256]{3,2,1,0:T(8,128)} all-to-all(f32[8,4,32,256]{3,2,1,0:T(8,128)S(1)} %shard_map.179._), channel_id=1, replica_groups=mesh['limb'=4,'coef'=8] {'coef'}, dimensions={0} | all-to-all | bytes 2097152 | tf_op jit(solution)/shard_map/all_to_all | solution.py:470
  259.5 18.8 %all_to_all.150.refs_1_ = f32[8,4,32,256]{3,2,1,0:T(8,128)S(1)} all-to-all(f32[8,4,32,256]{3,2,1,0:T(8,128)} %copy-done.18), channel_id=1, replica_groups=mesh['limb'=4,'coef'=8] {'coef'}, dimensions={0} | all-to-all | bytes 2097152 | tf_op jit(solution)/shard_map/all_to_all | solution.py:470
  278.3 48.8 %collective-permute-start.4 = (f32[8,4,32,256]{3,2,1,0:T(8,128)S(1)}, f32[8,4,32,256]{3,2,1,0:T(8,128)}, u32[]{:S(2)}, u32[]{:S(2)}) collective-permute-start(f32[8,4,32,256]{3,2,1,0:T(8,128)S(1)} %all_to_all.150.refs_1_), channel_id=1, source_target_pairs={{0,8},{24,16},{1,9},{25,17},{2,10},{26,18},{3,11},{27,19},{4,12},{... | collective-permute-start | bytes 3145736 | tf_op jit(solution)/shard_map/ppermute | solution.py:473
  330.6 12.3 %shard_map.180 = (f32[8,4,32,256]{3,2,1,0:T(8,128)S(1)}, f32[4,2,8,8192]{3,2,1,0:T(8,128)S(1)}) custom-call(f32[8,4,32,256]{3,2,1,0:T(8,128)S(1)} %copy-done.20, f32[2,12,16]{2,1,0:T(8,128)S(1)} %bitcast.43, f32[32,4,32,256]{3,2,1,0:T(8,128)S(1)} %copy-done.49, f32[12,32,256]{2,1,0:T(8,128)S(1)} %reshape.27.refs_2_, ...), custom_call_target="tpu_custom_call" | custom-call | flops 16000000 | tf_op jit(solution)/shard_map/pallas_call | solution.py:499
  351.1 20.6 %collective-permute-done.4.refs_2_ = f32[8,4,32,256]{3,2,1,0:T(8,128)} collective-permute-done((f32[8,4,32,256]{3,2,1,0:T(8,128)S(1)}, f32[8,4,32,256]{3,2,1,0:T(8,128)}, u32[]{:S(2)}, u32[]{:S(2)}) %collective-permute-start.4) | collective-permute-done | bytes 1048608 | tf_op jit(solution)/shard_map/ppermute | solution.py:473
  393.0 6.3 all-to-all-done.13.refs_0_
  403.7 18.4 %all_to_all.151 = f32[8,4,32,256]{3,2,1,0:T(8,128)} all-to-all(f32[8,4,32,256]{3,2,1,0:T(8,128)S(1)} %shard_map.184._), channel_id=1, replica_groups=mesh['limb'=4,'coef'=8] {'coef'}, dimensions={0} | all-to-all | bytes 2097152 | tf_op jit(solution)/shard_map/all_to_all | solution.py:470
  428.2 13.7 %all-to-all-done.16.refs_1_ = f32[8,4,32,256]{3,2,1,0:T(8,128)} async-done(((f32[8,4,32,256]{3,2,1,0:T(8,128)}), f32[8,4,32,256]{3,2,1,0:T(8,128)}, u32[]{:S(2)}, u32[]{:S(2)}) %all-to-all-start.16) | async-done | bytes 1048608 | tf_op jit(solution)/shard_map/all_to_all | solution.py:470
  441.8 40.3 %collective-permute-start.8 = (f32[8,4,32,256]{3,2,1,0:T(8,128)}, f32[8,4,32,256]{3,2,1,0:T(8,128)}, u32[]{:S(2)}, u32[]{:S(2)}) collective-permute-start(f32[8,4,32,256]{3,2,1,0:T(8,128)} %all-to-all-done.16.refs_1_), channel_id=1, source_target_pairs={{0,8},{24,16},{1,9},{25,17},{2,10},{26,18},{3,11},{27,19},{4,12},{... | collective-permute-start | bytes 3145736 | tf_op jit(solution)/shard_map/ppermute | solution.py:473
  486.6 58.7 %collective-permute-done.6.refs_5_ = f32[16,2,32,256]{3,2,1,0:T(8,128)} collective-permute-done((f32[16,2,32,256]{3,2,1,0:T(8,128)}, f32[16,2,32,256]{3,2,1,0:T(8,128)}, u32[]{:S(2)}, u32[]{:S(2)}) %collective-permute-start.6) | collective-permute-done | bytes 1048608 | tf_op jit(solution)/shard_map/ppermute | solution.py:479
  549.5 5.3 shard_map.185
  557.0 13.0 %shard_map.186 = (f32[8,4,32,256]{3,2,1,0:T(8,128)}, f32[4,2,8,8192]{3,2,1,0:T(8,128)S(1)}) custom-call(f32[8,128]{1,0:T(8,128)S(1)} %get-tuple-element.40._, f32[2,12,16]{2,1,0:T(8,128)S(1)} %bitcast.44, f32[32,4,32,256]{3,2,1,0:T(8,128)S(1)} %copy-done.50, f32[12,32,256]{2,1,0:T(8,128)S(1)} %reshape.27.refs_2_, ...), custom_call_target="tpu_custom_call" | custom-call | flops 16000000 | tf_op jit(solution)/shard_map/pallas_call | solution.py:499
  583.8 6.9 all-to-all-done.15.refs_0_
  604.2 6.4 all-to-all-done.17.refs_0_
  615.7 18.4 %all_to_all.152 = f32[8,4,32,256]{3,2,1,0:T(8,128)} all-to-all(f32[8,4,32,256]{3,2,1,0:T(8,128)S(1)} %shard_map.190._), channel_id=1, replica_groups=mesh['limb'=4,'coef'=8] {'coef'}, dimensions={0} | all-to-all | bytes 2097152 | tf_op jit(solution)/shard_map/all_to_all | solution.py:470
  635.5 19.6 %all_to_all.153.refs_1_ = f32[8,4,32,256]{3,2,1,0:T(8,128)} all-to-all(f32[8,4,32,256]{3,2,1,0:T(8,128)} %copy-done.17), channel_id=1, replica_groups=mesh['limb'=4,'coef'=8] {'coef'}, dimensions={0} | all-to-all | bytes 2097152 | tf_op jit(solution)/shard_map/all_to_all | solution.py:470
  655.0 24.5 %collective-permute-start.12 = (f32[8,4,32,256]{3,2,1,0:T(8,128)}, f32[8,4,32,256]{3,2,1,0:T(8,128)}, u32[]{:S(2)}, u32[]{:S(2)}) collective-permute-start(f32[8,4,32,256]{3,2,1,0:T(8,128)} %all_to_all.153.refs_1_), channel_id=1, source_target_pairs={{0,8},{24,16},{1,9},{25,17},{2,10},{26,18},{3,11},{27,19},{4,12},{... | collective-permute-start | bytes 3145736 | tf_op jit(solution)/shard_map/ppermute | solution.py:473
  681.0 89.9 %collective-permute-done.10.refs_5_ = f32[16,4,32,256]{3,2,1,0:T(8,128)S(1)} collective-permute-done((f32[16,4,32,256]{3,2,1,0:T(8,128)}, f32[16,4,32,256]{3,2,1,0:T(8,128)S(1)}, u32[]{:S(2)}, u32[]{:S(2)}) %collective-permute-start.10) | collective-permute-done | bytes 2097184 | tf_op jit(solution)/shard_map/ppermute | solution.py:479
  773.8 8.6 shard_map.191
  784.5 13.0 %shard_map.192 = (f32[8,4,32,256]{3,2,1,0:T(8,128)}, f32[4,2,8,8192]{3,2,1,0:T(8,128)S(1)}) custom-call(f32[8,128]{1,0:T(8,128)S(1)} %get-tuple-element.45._, f32[2,12,16]{2,1,0:T(8,128)S(1)} %bitcast.45, f32[32,4,32,256]{3,2,1,0:T(8,128)S(1)} %copy-done.48, f32[12,32,256]{2,1,0:T(8,128)S(1)} %reshape.27.refs_2_, ...), custom_call_target="tpu_custom_call" | custom-call | flops 16000000 | tf_op jit(solution)/shard_map/pallas_call | solution.py:499
  809.6 8.9 all-to-all-done.19.refs_0_
  842.0 8.7 shard_map.197
  852.9 12.3 %shard_map.198 = (f32[8,4,32,256]{3,2,1,0:T(8,128)S(1)}, f32[4,2,8,8192]{3,2,1,0:T(8,128)S(1)}) custom-call(f32[8,128]{1,0:T(8,128)S(1)} %get-tuple-element.50._, f32[2,12,16]{2,1,0:T(8,128)S(1)} %bitcast.46, f32[32,4,32,256]{3,2,1,0:T(8,128)S(1)} %copy-done.51, f32[12,32,256]{2,1,0:T(8,128)S(1)} %reshape.27.refs_2_, ...), custom_call_target="tpu_custom_call" | custom-call | flops 16000000 | tf_op jit(solution)/shard_map/pallas_call | solution.py:499
  866.6 19.3 %all_to_all.154.refs_0_ = f32[8,4,32,256]{3,2,1,0:T(8,128)} all-to-all(f32[8,4,32,256]{3,2,1,0:T(8,128)S(1)} %get-tuple-element.51._), channel_id=1, replica_groups=mesh['limb'=4,'coef'=8] {'coef'}, dimensions={0} | all-to-all | bytes 2097152 | tf_op jit(solution)/shard_map/all_to_all | solution.py:470
  894.9 9.9 all-to-all-done.24.refs_1_
  909.3 28.5 %collective-permute-start.16 = (f32[8,4,32,256]{3,2,1,0:T(8,128)}, f32[8,4,32,256]{3,2,1,0:T(8,128)}, u32[]{:S(2)}, u32[]{:S(2)}) collective-permute-start(f32[8,4,32,256]{3,2,1,0:T(8,128)} %copy-done.21), channel_id=1, source_target_pairs={{0,8},{24,16},{1,9},{25,17},{2,10},{26,18},{3,11},{27,19},{4,12},{... | collective-permute-start | bytes 3145736 | tf_op jit(solution)/shard_map/ppermute | solution.py:473
  939.1 14.0 %collective-permute-start.20 = (f32[8,4,32,256]{3,2,1,0:T(8,128)S(1)}, f32[8,4,32,256]{3,2,1,0:T(8,128)}, u32[]{:S(2)}, u32[]{:S(2)}) collective-permute-start(f32[8,4,32,256]{3,2,1,0:T(8,128)S(1)} %all-to-all-done.26.refs_1_), channel_id=1, source_target_pairs={{0,8},{24,16},{1,9},{25,17},{2,10},{26,18},{3,11},{27,19},{4,12},{... | collective-permute-start | bytes 3145736 | tf_op jit(solution)/shard_map/ppermute | solution.py:473
  953.8 26.5 %collective-permute-done.16.refs_2_ = f32[8,4,32,256]{3,2,1,0:T(8,128)} collective-permute-done((f32[8,4,32,256]{3,2,1,0:T(8,128)}, f32[8,4,32,256]{3,2,1,0:T(8,128)}, u32[]{:S(2)}, u32[]{:S(2)}) %collective-permute-start.16) | collective-permute-done | bytes 1048608 | tf_op jit(solution)/shard_map/ppermute | solution.py:473
  982.7 19.9 %collective-permute-done.20.refs_2_ = f32[8,4,32,256]{3,2,1,0:T(8,128)} collective-permute-done((f32[8,4,32,256]{3,2,1,0:T(8,128)S(1)}, f32[8,4,32,256]{3,2,1,0:T(8,128)}, u32[]{:S(2)}, u32[]{:S(2)}) %collective-permute-start.20) | collective-permute-done | bytes 1048608 | tf_op jit(solution)/shard_map/ppermute | solution.py:473
  1012.3 8.7 shard_map.201
  1025.3 6.6 shard_map.202
  1037.4 13.2 %all_to_all.155.refs_0_ = f32[8,2,32,256]{3,2,1,0:T(8,128)S(1)} all-to-all(f32[8,2,32,256]{3,2,1,0:T(8,128)S(1)} %get-tuple-element.56._), channel_id=1, replica_groups=mesh['limb'=4,'coef'=8] {'coef'}, dimensions={0} | all-to-all | bytes 1048576 | tf_op jit(solution)/shard_map/all_to_all | solution.py:470
  1051.2 12.1 %all_to_all.156.refs_1_ = f32[8,2,32,256]{3,2,1,0:T(8,128)S(1)} all-to-all(f32[8,2,32,256]{3,2,1,0:T(8,128)S(1)} %shard_map.204._), channel_id=1, replica_groups=mesh['limb'=4,'coef'=8] {'coef'}, dimensions={0} | all-to-all | bytes 1048576 | tf_op jit(solution)/shard_map/all_to_all | solution.py:470
  1063.4 25.6 %collective-permute-start.25 = (f32[8,2,32,256]{3,2,1,0:T(8,128)S(1)}, f32[8,2,32,256]{3,2,1,0:T(8,128)S(1)}, u32[]{:S(2)}, u32[]{:S(2)}) collective-permute-start(f32[8,2,32,256]{3,2,1,0:T(8,128)S(1)} %all_to_all.156.refs_1_), channel_id=1, source_target_pairs={{0,8},{24,16},{1,9},{25,17},{2,10},{26,18},{3,11},{27,19},{4,12},{... | collective-permute-start | bytes 1572872 | tf_op jit(solution)/shard_map/ppermute | solution.py:473
  1089.6 9.9 collective-permute-done.25.refs_2_
  1100.5 8.7 shard_map.205
  1109.2 8.7 shard_map.206
  1121.0 26.9 %collective-permute-done.27.refs_5_ = f32[16,2,32,256]{3,2,1,0:T(8,128)S(1)} collective-permute-done((f32[16,2,32,256]{3,2,1,0:T(8,128)S(1)}, f32[16,2,32,256]{3,2,1,0:T(8,128)S(1)}, u32[]{:S(2)}, u32[]{:S(2)}) %collective-permute-start.27) | collective-permute-done | bytes 1048608 | tf_op jit(solution)/shard_map/ppermute | solution.py:479
  (321 shorter events, 292.1 us)
Async XLA Ops:
  13.4 14.9 %all-to-all-start = ((f32[8,2,32,256]{3,2,1,0:T(8,128)}), f32[8,2,32,256]{3,2,1,0:T(8,128)S(1)}, u32[]{:S(2)}, u32[]{:S(2)}) async-start(f32[8,2,32,256]{3,2,1,0:T(8,128)} %shard_map.167._), calls=%async_computation | async-start | bytes 1048576 | tf_op jit(solution)/shard_map/all_to_all | solution.py:470
  18.6 89.4 %all-gather.8.cloned.1.call-start = ((), (), s32[]{:S(2)}) async-start(), calls=%async_computation.29 | async-start | bytes 2621440 | tf_op jit(solution)/shard_map/all_gather | solution.py:523
  41.8 139.1 %all-gather.10.cloned.1.call-start = ((), (), s32[]{:S(2)}) async-start(), calls=%async_computation.30 | async-start | bytes 5242880 | tf_op jit(solution)/shard_map/all_gather | solution.py:523
  134.8 18.9 %all-to-all-start.5 = ((f32[8,4,32,256]{3,2,1,0:T(8,128)}), f32[8,4,32,256]{3,2,1,0:T(8,128)S(1)}, u32[]{:S(2)}, u32[]{:S(2)}) async-start(f32[8,4,32,256]{3,2,1,0:T(8,128)} %shard_map.172._), calls=%async_computation.5 | async-start | bytes 2097152 | tf_op jit(solution)/shard_map/all_to_all | solution.py:470
  138.4 188.8 %all-gather.12.cloned.1.call-start = ((), (), s32[]{:S(2)}) async-start(), calls=%async_computation.31 | async-start | bytes 5242880 | tf_op jit(solution)/shard_map/all_gather | solution.py:523
  176.6 21.3 %all-to-all-start.8 = ((f32[8,2,32,256]{3,2,1,0:T(8,128)}), f32[8,2,32,256]{3,2,1,0:T(8,128)}, u32[]{:S(2)}, u32[]{:S(2)}) async-start(f32[8,2,32,256]{3,2,1,0:T(8,128)} %copy-done.30), calls=%async_computation.8 | async-start | bytes 1048576 | tf_op jit(solution)/shard_map/all_to_all | solution.py:470
  197.9 19.5 %all-to-all-start.7 = ((f32[8,4,32,256]{3,2,1,0:T(8,128)}), f32[8,4,32,256]{3,2,1,0:T(8,128)S(1)}, u32[]{:S(2)}, u32[]{:S(2)}) async-start(f32[8,4,32,256]{3,2,1,0:T(8,128)} %copy-done.36), calls=%async_computation.7 | async-start | bytes 2097152 | tf_op jit(solution)/shard_map/all_to_all | solution.py:470
  202.0 27.3 %collective-permute-start.1 = (f32[8,2,32,256]{3,2,1,0:T(8,128)}, f32[8,2,32,256]{3,2,1,0:T(8,128)}, u32[]{:S(2)}, u32[]{:S(2)}) collective-permute-start(f32[8,2,32,256]{3,2,1,0:T(8,128)} %all-to-all-done.8.refs_1_), channel_id=1, source_target_pairs={{0,8},{24,16},{1,9},{25,17},{2,10},{26,18},{3,11},{27,19},{4,12},{... | collective-permute-start | bytes 1572872 | tf_op jit(solution)/shard_map/ppermute | solution.py:473
  217.4 19.6 %all-to-all-start.9 = ((f32[8,4,32,256]{3,2,1,0:T(8,128)}), f32[8,4,32,256]{3,2,1,0:T(8,128)}, u32[]{:S(2)}, u32[]{:S(2)}) async-start(f32[8,4,32,256]{3,2,1,0:T(8,128)} %shard_map.176._), calls=%async_computation.9 | async-start | bytes 2097152 | tf_op jit(solution)/shard_map/all_to_all | solution.py:470
  221.6 333.2 %all-gather.14.cloned.1.call-start = ((), (), s32[]{:S(2)}) async-start(), calls=%async_computation.32 | async-start | bytes 5242880 | tf_op jit(solution)/shard_map/all_gather | solution.py:523
  278.3 93.4 %collective-permute-start.4 = (f32[8,4,32,256]{3,2,1,0:T(8,128)S(1)}, f32[8,4,32,256]{3,2,1,0:T(8,128)}, u32[]{:S(2)}, u32[]{:S(2)}) collective-permute-start(f32[8,4,32,256]{3,2,1,0:T(8,128)S(1)} %all_to_all.150.refs_1_), channel_id=1, source_target_pairs={{0,8},{24,16},{1,9},{25,17},{2,10},{26,18},{3,11},{27,19},{4,12},{... | collective-permute-start | bytes 3145736 | tf_op jit(solution)/shard_map/ppermute | solution.py:473
  345.2 34.5 %all-to-all-start.11 = ((f32[8,4,32,256]{3,2,1,0:T(8,128)}), f32[8,4,32,256]{3,2,1,0:T(8,128)}, u32[]{:S(2)}, u32[]{:S(2)}) async-start(f32[8,4,32,256]{3,2,1,0:T(8,128)} %copy-done.32), calls=%async_computation.11 | async-start | bytes 2097152 | tf_op jit(solution)/shard_map/all_to_all | solution.py:470
  349.4 37.3 %collective-permute-start.3 = (f32[8,4,32,256]{3,2,1,0:T(8,128)S(1)}, f32[8,4,32,256]{3,2,1,0:T(8,128)}, u32[]{:S(2)}, u32[]{:S(2)}) collective-permute-start(f32[8,4,32,256]{3,2,1,0:T(8,128)S(1)} %all_to_all.150.refs_1_), channel_id=1, source_target_pairs={{8,16},{16,8},{9,17},{17,9},{10,18},{18,10},{11,19},{19,11},{12,20... | collective-permute-start | bytes 3145736 | tf_op jit(solution)/shard_map/ppermute | solution.py:476
  371.7 15.1 %collective-permute-start.5 = (f32[8,4,32,256]{3,2,1,0:T(8,128)}, f32[8,4,32,256]{3,2,1,0:T(8,128)}, u32[]{:S(2)}, u32[]{:S(2)}) collective-permute-start(f32[8,4,32,256]{3,2,1,0:T(8,128)} %collective-permute-done.4.refs_2_), channel_id=1, source_target_pairs={{8,16},{16,8},{9,17},{17,9},{10,18},{18,10},{11,19},{19,11},{12,20... | collective-permute-start | bytes 3145736 | tf_op jit(solution)/shard_map/ppermute | solution.py:476
  379.7 19.6 %all-to-all-start.13 = ((f32[8,4,32,256]{3,2,1,0:T(8,128)}), f32[8,4,32,256]{3,2,1,0:T(8,128)}, u32[]{:S(2)}, u32[]{:S(2)}) async-start(f32[8,4,32,256]{3,2,1,0:T(8,128)} %shard_map.181._), calls=%async_computation.13 | async-start | bytes 2097152 | tf_op jit(solution)/shard_map/all_to_all | solution.py:470
  383.9 398.4 %all-gather.16.cloned.1.call-start = ((), (), s32[]{:S(2)}) async-start(), calls=%async_computation.33 | async-start | bytes 5242880 | tf_op jit(solution)/shard_map/all_gather | solution.py:523
  422.2 19.7 %all-to-all-start.16 = ((f32[8,4,32,256]{3,2,1,0:T(8,128)}), f32[8,4,32,256]{3,2,1,0:T(8,128)}, u32[]{:S(2)}, u32[]{:S(2)}) async-start(f32[8,4,32,256]{3,2,1,0:T(8,128)} %copy-done.14), calls=%async_computation.16 | async-start | bytes 2097152 | tf_op jit(solution)/shard_map/all_to_all | solution.py:470
  426.4 118.9 %collective-permute-start.6 = (f32[16,2,32,256]{3,2,1,0:T(8,128)}, f32[16,2,32,256]{3,2,1,0:T(8,128)}, u32[]{:S(2)}, u32[]{:S(2)}) collective-permute-start(f32[16,2,32,256]{3,2,1,0:T(8,128)} %copy-done.45), channel_id=1, source_target_pairs={{8,0},{16,24},{9,1},{17,25},{10,2},{18,26},{11,3},{19,27},{12,4},{... | collective-permute-start | bytes 3145736 | tf_op jit(solution)/shard_map/ppermute | solution.py:479
  441.8 135.2 %collective-permute-start.8 = (f32[8,4,32,256]{3,2,1,0:T(8,128)}, f32[8,4,32,256]{3,2,1,0:T(8,128)}, u32[]{:S(2)}, u32[]{:S(2)}) collective-permute-start(f32[8,4,32,256]{3,2,1,0:T(8,128)} %all-to-all-done.16.refs_1_), channel_id=1, source_target_pairs={{0,8},{24,16},{1,9},{25,17},{2,10},{26,18},{3,11},{27,19},{4,12},{... | collective-permute-start | bytes 3145736 | tf_op jit(solution)/shard_map/ppermute | solution.py:473
  571.4 19.4 %all-to-all-start.15 = ((f32[8,4,32,256]{3,2,1,0:T(8,128)}), f32[8,4,32,256]{3,2,1,0:T(8,128)S(1)}, u32[]{:S(2)}, u32[]{:S(2)}) async-start(f32[8,4,32,256]{3,2,1,0:T(8,128)} %get-tuple-element.41._), calls=%async_computation.15 | async-start | bytes 2097152 | tf_op jit(solution)/shard_map/all_to_all | solution.py:470
  575.4 22.4 %collective-permute-start.7 = (f32[8,4,32,256]{3,2,1,0:T(8,128)}, f32[8,4,32,256]{3,2,1,0:T(8,128)}, u32[]{:S(2)}, u32[]{:S(2)}) collective-permute-start(f32[8,4,32,256]{3,2,1,0:T(8,128)} %all-to-all-done.16.refs_1_), channel_id=1, source_target_pairs={{8,16},{16,8},{9,17},{17,9},{10,18},{18,10},{11,19},{19,11},{12,20... | collective-permute-start | bytes 3145736 | tf_op jit(solution)/shard_map/ppermute | solution.py:476
  577.0 20.8 %collective-permute-start.9 = (f32[8,4,32,256]{3,2,1,0:T(8,128)}, f32[8,4,32,256]{3,2,1,0:T(8,128)}, u32[]{:S(2)}, u32[]{:S(2)}) collective-permute-start(f32[8,4,32,256]{3,2,1,0:T(8,128)} %collective-permute-done.8.refs_2_), channel_id=1, source_target_pairs={{8,16},{16,8},{9,17},{17,9},{10,18},{18,10},{11,19},{19,11},{12,20... | collective-permute-start | bytes 3145736 | tf_op jit(solution)/shard_map/ppermute | solution.py:476
  591.7 18.9 %all-to-all-start.17 = ((f32[8,4,32,256]{3,2,1,0:T(8,128)}), f32[8,4,32,256]{3,2,1,0:T(8,128)S(1)}, u32[]{:S(2)}, u32[]{:S(2)}) async-start(f32[8,4,32,256]{3,2,1,0:T(8,128)} %shard_map.187._), calls=%async_computation.17 | async-start | bytes 2097152 | tf_op jit(solution)/shard_map/all_to_all | solution.py:470
  595.3 255.4 %all-gather.18.cloned.1.call-start = ((), (), s32[]{:S(2)}) async-start(), calls=%async_computation.34 | async-start | bytes 5242880 | tf_op jit(solution)/shard_map/all_gather | solution.py:523
  634.2 136.8 %collective-permute-start.10 = (f32[16,4,32,256]{3,2,1,0:T(8,128)}, f32[16,4,32,256]{3,2,1,0:T(8,128)S(1)}, u32[]{:S(2)}, u32[]{:S(2)}) collective-permute-start(f32[16,4,32,256]{3,2,1,0:T(8,128)} %copy-done.24), channel_id=1, source_target_pairs={{8,0},{16,24},{9,1},{17,25},{10,2},{18,26},{11,3},{19,27},{12,4},{... | collective-permute-start | bytes 6291464 | tf_op jit(solution)/shard_map/ppermute | solution.py:479
  655.0 148.8 %collective-permute-start.12 = (f32[8,4,32,256]{3,2,1,0:T(8,128)}, f32[8,4,32,256]{3,2,1,0:T(8,128)}, u32[]{:S(2)}, u32[]{:S(2)}) collective-permute-start(f32[8,4,32,256]{3,2,1,0:T(8,128)} %all_to_all.153.refs_1_), channel_id=1, source_target_pairs={{0,8},{24,16},{1,9},{25,17},{2,10},{26,18},{3,11},{27,19},{4,12},{... | collective-permute-start | bytes 3145736 | tf_op jit(solution)/shard_map/ppermute | solution.py:473
  679.6 160.8 %collective-permute-start.14 = (f32[16,4,32,256]{3,2,1,0:T(8,128)}, f32[16,4,32,256]{3,2,1,0:T(8,128)}, u32[]{:S(2)}, u32[]{:S(2)}) collective-permute-start(f32[16,4,32,256]{3,2,1,0:T(8,128)} %copy-done.26), channel_id=1, source_target_pairs={{8,0},{16,24},{9,1},{17,25},{10,2},{18,26},{11,3},{19,27},{12,4},{... | collective-permute-start | bytes 6291464 | tf_op jit(solution)/shard_map/ppermute | solution.py:479
  798.9 19.6 %all-to-all-start.19 = ((f32[8,4,32,256]{3,2,1,0:T(8,128)}), f32[8,4,32,256]{3,2,1,0:T(8,128)}, u32[]{:S(2)}, u32[]{:S(2)}) async-start(f32[8,4,32,256]{3,2,1,0:T(8,128)} %get-tuple-element.46._), calls=%async_computation.19 | async-start | bytes 2097152 | tf_op jit(solution)/shard_map/all_to_all | solution.py:470
  803.1 23.5 %collective-permute-start.11 = (f32[8,4,32,256]{3,2,1,0:T(8,128)}, f32[8,4,32,256]{3,2,1,0:T(8,128)S(1)}, u32[]{:S(2)}, u32[]{:S(2)}) collective-permute-start(f32[8,4,32,256]{3,2,1,0:T(8,128)} %all_to_all.153.refs_1_), channel_id=1, source_target_pairs={{8,16},{16,8},{9,17},{17,9},{10,18},{18,10},{11,19},{19,11},{12,20... | collective-permute-start | bytes 3145736 | tf_op jit(solution)/shard_map/ppermute | solution.py:476
  803.9 22.7 %collective-permute-start.13 = (f32[8,4,32,256]{3,2,1,0:T(8,128)}, f32[8,4,32,256]{3,2,1,0:T(8,128)}, u32[]{:S(2)}, u32[]{:S(2)}) collective-permute-start(f32[8,4,32,256]{3,2,1,0:T(8,128)} %collective-permute-done.12.refs_2_), channel_id=1, source_target_pairs={{8,16},{16,8},{9,17},{17,9},{10,18},{18,10},{11,19},{19,11},{12,20... | collective-permute-start | bytes 3145736 | tf_op jit(solution)/shard_map/ppermute | solution.py:476
  818.5 13.9 %all-to-all-start.21 = ((f32[8,2,32,256]{3,2,1,0:T(8,128)}), f32[8,2,32,256]{3,2,1,0:T(8,128)}, u32[]{:S(2)}, u32[]{:S(2)}) async-start(f32[8,2,32,256]{3,2,1,0:T(8,128)} %shard_map.193._), calls=%async_computation.21 | async-start | bytes 1048576 | tf_op jit(solution)/shard_map/all_to_all | solution.py:470
  836.2 30.3 %all-to-all-start.25 = ((f32[8,2,32,256]{3,2,1,0:T(8,128)}), f32[8,2,32,256]{3,2,1,0:T(8,128)}, u32[]{:S(2)}, u32[]{:S(2)}) async-start(f32[8,2,32,256]{3,2,1,0:T(8,128)} %shard_map.196._), calls=%async_computation.25 | async-start | bytes 1048576 | tf_op jit(solution)/shard_map/all_to_all | solution.py:470
  885.9 18.9 %all-to-all-start.24 = ((f32[8,4,32,256]{3,2,1,0:T(8,128)}), f32[8,4,32,256]{3,2,1,0:T(8,128)S(1)}, u32[]{:S(2)}, u32[]{:S(2)}) async-start(f32[8,4,32,256]{3,2,1,0:T(8,128)} %shard_map.194._), calls=%async_computation.24 | async-start | bytes 2097152 | tf_op jit(solution)/shard_map/all_to_all | solution.py:470
  889.4 131.5 %all-gather.20.cloned.1.call-start = ((), (), s32[]{:S(2)}) async-start(), calls=%async_computation.35 | async-start | bytes 2621440 | tf_op jit(solution)/shard_map/all_gather | solution.py:523
  905.8 33.3 %all-to-all-start.26 = ((f32[8,4,32,256]{3,2,1,0:T(8,128)}), f32[8,4,32,256]{3,2,1,0:T(8,128)S(1)}, u32[]{:S(2)}, u32[]{:S(2)}) async-start(f32[8,4,32,256]{3,2,1,0:T(8,128)} %copy-done.15), calls=%async_computation.26 | async-start | bytes 2097152 | tf_op jit(solution)/shard_map/all_to_all | solution.py:470
  909.3 71.0 %collective-permute-start.16 = (f32[8,4,32,256]{3,2,1,0:T(8,128)}, f32[8,4,32,256]{3,2,1,0:T(8,128)}, u32[]{:S(2)}, u32[]{:S(2)}) collective-permute-start(f32[8,4,32,256]{3,2,1,0:T(8,128)} %copy-done.21), channel_id=1, source_target_pairs={{0,8},{24,16},{1,9},{25,17},{2,10},{26,18},{3,11},{27,19},{4,12},{... | collective-permute-start | bytes 3145736 | tf_op jit(solution)/shard_map/ppermute | solution.py:473
  937.8 74.4 %collective-permute-start.18 = (f32[16,4,32,256]{3,2,1,0:T(8,128)}, f32[16,4,32,256]{3,2,1,0:T(8,128)}, u32[]{:S(2)}, u32[]{:S(2)}) collective-permute-start(f32[16,4,32,256]{3,2,1,0:T(8,128)} %copy-done.28), channel_id=1, source_target_pairs={{8,0},{16,24},{9,1},{17,25},{10,2},{18,26},{11,3},{19,27},{12,4},{... | collective-permute-start | bytes 6291464 | tf_op jit(solution)/shard_map/ppermute | solution.py:479
  939.1 63.4 %collective-permute-start.20 = (f32[8,4,32,256]{3,2,1,0:T(8,128)S(1)}, f32[8,4,32,256]{3,2,1,0:T(8,128)}, u32[]{:S(2)}, u32[]{:S(2)}) collective-permute-start(f32[8,4,32,256]{3,2,1,0:T(8,128)S(1)} %all-to-all-done.26.refs_1_), channel_id=1, source_target_pairs={{0,8},{24,16},{1,9},{25,17},{2,10},{26,18},{3,11},{27,19},{4,12},{... | collective-permute-start | bytes 3145736 | tf_op jit(solution)/shard_map/ppermute | solution.py:473
  953.1 51.1 %collective-permute-start.15 = (f32[8,4,32,256]{3,2,1,0:T(8,128)}, f32[8,4,32,256]{3,2,1,0:T(8,128)S(1)}, u32[]{:S(2)}, u32[]{:S(2)}) collective-permute-start(f32[8,4,32,256]{3,2,1,0:T(8,128)} %copy-done.21), channel_id=1, source_target_pairs={{8,16},{16,8},{9,17},{17,9},{10,18},{18,10},{11,19},{19,11},{12,20... | collective-permute-start | bytes 3145736 | tf_op jit(solution)/shard_map/ppermute | solution.py:476
  980.3 23.9 %collective-permute-start.17 = (f32[8,4,32,256]{3,2,1,0:T(8,128)}, f32[8,4,32,256]{3,2,1,0:T(8,128)S(1)}, u32[]{:S(2)}, u32[]{:S(2)}) collective-permute-start(f32[8,4,32,256]{3,2,1,0:T(8,128)} %collective-permute-done.16.refs_2_), channel_id=1, source_target_pairs={{8,16},{16,8},{9,17},{17,9},{10,18},{18,10},{11,19},{19,11},{12,20... | collective-permute-start | bytes 3145736 | tf_op jit(solution)/shard_map/ppermute | solution.py:476
  981.0 50.9 %collective-permute-start.19 = (f32[8,4,32,256]{3,2,1,0:T(8,128)S(1)}, f32[8,4,32,256]{3,2,1,0:T(8,128)}, u32[]{:S(2)}, u32[]{:S(2)}) collective-permute-start(f32[8,4,32,256]{3,2,1,0:T(8,128)S(1)} %all-to-all-done.26.refs_1_), channel_id=1, source_target_pairs={{8,16},{16,8},{9,17},{17,9},{10,18},{18,10},{11,19},{19,11},{12,20... | collective-permute-start | bytes 3145736 | tf_op jit(solution)/shard_map/ppermute | solution.py:476
  1002.5 29.4 %collective-permute-start.21 = (f32[8,4,32,256]{3,2,1,0:T(8,128)}, f32[8,4,32,256]{3,2,1,0:T(8,128)}, u32[]{:S(2)}, u32[]{:S(2)}) collective-permute-start(f32[8,4,32,256]{3,2,1,0:T(8,128)} %collective-permute-done.20.refs_2_), channel_id=1, source_target_pairs={{8,16},{16,8},{9,17},{17,9},{10,18},{18,10},{11,19},{19,11},{12,20... | collective-permute-start | bytes 3145736 | tf_op jit(solution)/shard_map/ppermute | solution.py:476
  1010.9 89.5 %collective-permute-start.22 = (f32[16,4,32,256]{3,2,1,0:T(8,128)}, f32[16,4,32,256]{3,2,1,0:T(8,128)}, u32[]{:S(2)}, u32[]{:S(2)}) collective-permute-start(f32[16,4,32,256]{3,2,1,0:T(8,128)} %shard_map.200._), channel_id=1, source_target_pairs={{8,0},{16,24},{9,1},{17,25},{10,2},{18,26},{11,3},{19,27},{12,4},{... | collective-permute-start | bytes 6291464 | tf_op jit(solution)/shard_map/ppermute | solution.py:479
  1035.8 73.3 %collective-permute-start.23 = (f32[16,4,32,256]{3,2,1,0:T(8,128)S(1)}, f32[16,4,32,256]{3,2,1,0:T(8,128)S(1)}, u32[]{:S(2)}, u32[]{:S(2)}) collective-permute-start(f32[16,4,32,256]{3,2,1,0:T(8,128)S(1)} %shard_map.203._), channel_id=1, source_target_pairs={{8,0},{16,24},{9,1},{17,25},{10,2},{18,26},{11,3},{19,27},{12,4},{... | collective-permute-start | bytes 6291464 | tf_op jit(solution)/shard_map/ppermute | solution.py:479
  1063.4 36.1 %collective-permute-start.25 = (f32[8,2,32,256]{3,2,1,0:T(8,128)S(1)}, f32[8,2,32,256]{3,2,1,0:T(8,128)S(1)}, u32[]{:S(2)}, u32[]{:S(2)}) collective-permute-start(f32[8,2,32,256]{3,2,1,0:T(8,128)S(1)} %all_to_all.156.refs_1_), channel_id=1, source_target_pairs={{0,8},{24,16},{1,9},{25,17},{2,10},{26,18},{3,11},{27,19},{4,12},{... | collective-permute-start | bytes 1572872 | tf_op jit(solution)/shard_map/ppermute | solution.py:473
  1088.9 29.0 %collective-permute-start.24 = (f32[8,2,32,256]{3,2,1,0:T(8,128)S(1)}, f32[8,2,32,256]{3,2,1,0:T(8,128)S(1)}, u32[]{:S(2)}, u32[]{:S(2)}) collective-permute-start(f32[8,2,32,256]{3,2,1,0:T(8,128)S(1)} %all_to_all.156.refs_1_), channel_id=1, source_target_pairs={{8,16},{16,8},{9,17},{17,9},{10,18},{18,10},{11,19},{19,11},{12,20... | collective-permute-start | bytes 1572872 | tf_op jit(solution)/shard_map/ppermute | solution.py:476
  1099.5 18.4 %collective-permute-start.26 = (f32[8,2,32,256]{3,2,1,0:T(8,128)S(1)}, f32[8,2,32,256]{3,2,1,0:T(8,128)S(1)}, u32[]{:S(2)}, u32[]{:S(2)}) collective-permute-start(f32[8,2,32,256]{3,2,1,0:T(8,128)S(1)} %collective-permute-done.25.refs_2_), channel_id=1, source_target_pairs={{8,16},{16,8},{9,17},{17,9},{10,18},{18,10},{11,19},{19,11},{12,20... | collective-permute-start | bytes 1572872 | tf_op jit(solution)/shard_map/ppermute | solution.py:476
  1119.7 28.2 %collective-permute-start.27 = (f32[16,2,32,256]{3,2,1,0:T(8,128)S(1)}, f32[16,2,32,256]{3,2,1,0:T(8,128)S(1)}, u32[]{:S(2)}, u32[]{:S(2)}) collective-permute-start(f32[16,2,32,256]{3,2,1,0:T(8,128)S(1)} %shard_map.207._), channel_id=1, source_target_pairs={{8,0},{16,24},{9,1},{17,25},{10,2},{18,26},{11,3},{19,27},{12,4},{... | collective-permute-start | bytes 3145736 | tf_op jit(solution)/shard_map/ppermute | solution.py:479
  (89 other events, 836.9 us)
Sparse Core Ops, SparseCore 0:
  41.9 45.0 all-gather.7
  88.5 79.5 all-gather.9
  176.8 91.4 all-gather.11
  269.7 134.1 all-gather.13
  422.3 134.3 all-gather.15
  634.3 129.7 all-gather.17
  891.8 85.7 all-gather.19

commit v2 on v1

--- a/solution.py
+++ b/solution.py
@@ -12,6 +12,7 @@
 ROWS = 256
 COLS = 256
 SIZES = (2, 4, 4, 4, 4, 4, 2)
+PER = 2
 F32 = jnp.float32
 BF16 = jnp.bfloat16
 
@@ -139,18 +140,22 @@
 
 def first_kernel(x, tw, wh, wl, out, scr, *, rows, cols):
     limbs = x.shape[1]
-    stacked = jnp.concatenate([x[0, :, r * cols : (r + 1) * cols] for r in range(rows)], axis=0)
-    put(scr, mm3(split(stacked), (wh[...], wl[...])) * tw[...])
     half = scr.shape[2]
-    for d in range(limbs):
-        for h in range(scr.shape[0]):
-            out[d, 0, :, h * half : (h + 1) * half] = scr[h, pl.ds(d, rows, stride=limbs), :]
+    for c in range(x.shape[0]):
+        stacked = jnp.concatenate(
+            [x[c, :, r * cols : (r + 1) * cols] for r in range(rows)], axis=0
+        )
+        put(scr, mm3(split(stacked), (wh[...], wl[...])) * tw[...])
+        for d in range(limbs):
+            for h in range(scr.shape[0]):
+                out[d, c, :, h * half : (h + 1) * half] = scr[h, pl.ds(d, rows, stride=limbs), :]
 
 
 def middle_kernel(x, mh, ml, out):
-    n, _, rows, cols = x.shape
-    y = mm3((mh[...], ml[...]), split(x[...].reshape(n * rows, cols)))
-    out[...] = y.reshape(n, 1, rows, cols)
+    n, cts, rows, cols = x.shape
+    for c in range(cts):
+        y = mm3((mh[...], ml[...]), split(x[:, c].reshape(n * rows, cols)))
+        out[:, c] = y.reshape(n, rows, cols)
 
 
 GROUP = 4
@@ -356,8 +361,8 @@
     def whole(x):
         return pl.BlockSpec(x.shape, lambda c: (0,) * x.ndim)
 
-    def polys(count):
-        return pl.BlockSpec((count, 1, rows, cols), lambda c: (0, c, 0, 0))
+    def polys(count, cts=1):
+        return pl.BlockSpec((count, cts, rows, cols), lambda c: (0, c, 0, 0))
 
     def stacked(count, size):
         return jax.ShapeDtypeStruct((count, size, rows, cols), F32)
@@ -374,7 +379,7 @@
             scratch_shapes=scratch,
             out_shape=out_shape,
             compiler_params=pltpu.CompilerParams(
-                dimension_semantics=("arbitrary",), vmem_limit_bytes=40 * 1024 * 1024
+                dimension_semantics=("arbitrary",), vmem_limit_bytes=60 * 1024 * 1024
             ),
             cost_estimate=pl.CostEstimate(
                 flops=int(flops * size), transcendentals=0, bytes_accessed=0
@@ -383,27 +388,29 @@
         )
 
     def first(start, size):
+        per = PER if start % PER == 0 and size % PER == 0 else 1
         return call(
             functools.partial(first_kernel, rows=rows, cols=cols),
-            size,
+            size // per,
             [
-                pl.BlockSpec((1, main, positions), lambda c: (start + c, 0, 0)),
+                pl.BlockSpec((per, main, positions), lambda c: (start // per + c, 0, 0)),
                 whole(tw_in),
                 whole(ic[0]),
                 whole(ic[1]),
             ],
-            polys(n),
+            polys(n, per),
             stacked(n, size),
             [pltpu.VMEM((lanes, rows * main, half), F32)],
-            1e6,
+            2e6,
         )
 
     def middle(size):
+        per = PER if size % PER == 0 else 1
         return call(
             middle_kernel,
-            size,
-            [polys(n), whole(merged[0]), whole(merged[1])],
-            polys(n),
+            size // per,
+            [polys(n, per), whole(merged[0]), whole(merged[1])],
+            polys(n, per),
             stacked(n, size),
             [],
             1e6,
@@ -534,12 +541,17 @@
     return tuple(outs)
 
 
+AHEAD = 3
+
+
 def schedule(n):
-    order = [(0, "A"), (0, "B"), (1, "A"), (1, "B")]
+    order = [(c, stage) for c in range(AHEAD) for stage in "AB"]
     for s in range(n - 1):
-        order += [(s, "D"), (s + 2, "A"), (s, "E"), (s - 1, "F"), (s + 2, "B"), (s - 2, "G")]
+        order += [(s, "D"), (s + AHEAD, "A"), (s, "E"), (s - 3, "G"), (s - 1, "F")]
+        order += [(s + AHEAD, "B")]
     s = n - 1
-    order += [(s, "D"), (s - 1, "F"), (s, "E"), (s - 2, "G"), (s - 1, "G"), (s, "F"), (s, "G")]
+    order += [(s, "D"), (s - 1, "F"), (s, "E"), (s - 3, "G"), (s - 2, "G"), (s, "F")]
+    order += [(s - 1, "G"), (s, "G")]
     return [(c, stage) for c, stage in order if 0 <= c < n]
 
 

time: 1170 us -> 1040 us (0.89)
  local copies, waits for them, and re-layouts: 114 us -> 22.7 us
  waiting for transfers between devices: 350 us -> 262 us
  Pallas kernels: 190 us -> 229 us
  starting transfers between devices: 283 us -> 304 us
  blocking collectives: 206 us -> 189 us
    ppermute x7, waiting for transfers between devices: 176 us -> 56.7 us  [outward(): return lax.ppermute(x, 'limb', [(1, 0), (2, 3)])]
    unnamed x177 -> x63, local copies, waits for them, and re-layouts: 94.1 us -> 8.19 us
    ppermute x7, waiting for transfers between devices: 83 us -> 111 us  [inward(): return lax.ppermute(x, 'limb', [(0, 1), (3, 2)])]
    all_to_all x12 -> x10, blocking collectives: 206 us -> 189 us  [exchange(): return lax.all_to_all(x, 'coef', split_axis=0, concat_axis=0, tiled=True)]
    ppermute x7, starting transfers between devices: 186 us -> 202 us  [inward(): return lax.ppermute(x, 'limb', [(0, 1), (3, 2)])]
    pallas_call x14, Pallas kernels: 23.9 us -> 36.6 us  [fast(): token = y = middle(size)(token, st['x'], *merged)]
    all_to_all x16 -> x18, starting transfers between devices: 64.7 us -> 72.2 us  [exchange(): return lax.all_to_all(x, 'coef', split_axis=0, concat_axis=0, tiled=True)]
    all_to_all x16 -> x18, waiting for transfers between devices: 83.1 us -> 88.5 us  [exchange(): return lax.all_to_all(x, 'coef', split_axis=0, concat_axis=0, tiled=True)]
  transfers between devices with their start and end apart: 52 -> 54, of which waited for: 21 -> 22; matrix products, arithmetic and copies ran while one was open for 2% -> 2% of each run, Pallas kernels for 16% -> 21%
where the time goes in v2:
time: 1040 us; the launch traced here: 1030 us
  starting transfers between devices  304 us (29%)
  waiting for transfers between devices  262 us (25%)
  Pallas kernels  229 us (22%)
  blocking collectives  189 us (18%)
  local copies, waits for them, and re-layouts  22.7 us (2%)
  between operations  15.1 us (1%)
    ppermute x7, starting transfers between devices, inward(): return lax.ppermute(x, 'limb', [(0, 1), (3, 2)])  202 us
    all_to_all x10, blocking collectives, exchange(): return lax.all_to_all(x, 'coef', split_axis=0, concat_axis=0, tiled=True)  189 us
    ppermute x7, waiting for transfers between devices, inward(): return lax.ppermute(x, 'limb', [(0, 1), (3, 2)])  111 us
    all_to_all x18, waiting for transfers between devices, exchange(): return lax.all_to_all(x, 'coef', split_axis=0, concat_axis=0, tiled=True)  88.5 us
    pallas_call x7, Pallas kernels, fast(): keyed(start, size)  84.7 us
    all_to_all x18, starting transfers between devices, exchange(): return lax.all_to_all(x, 'coef', split_axis=0, concat_axis=0, tiled=True)  72.2 us
    pallas_call x7, Pallas kernels, fast(): last(outs, start, size)  57.4 us
    ppermute x7, waiting for transfers between devices, outward(): return lax.ppermute(x, 'limb', [(1, 0), (2, 3)])  56.7 us
  transfers between devices with their start and end apart: 54, of which 22 were waited for; matrix products, arithmetic and copies ran while one was open for 2% of the time, Pallas kernels for 21%

profile of v2, /device:TPU:0, one launch (start us, length us, event | category | flops | bytes accessed | tf_op | source)
XLA Modules:
  0.0 1027.7 jit_solution(13011679333403485267)
XLA Ops:
  19.8 8.4 all-to-all-done.refs_0_
  31.2 13.8 %all_to_all.145 = f32[8,2,32,256]{3,2,1,0:T(8,128)} all-to-all(f32[8,2,32,256]{3,2,1,0:T(8,128)} %shard_map.168._), channel_id=1, replica_groups=mesh['limb'=4,'coef'=8] {'coef'}, dimensions={0} | all-to-all | bytes 1048576 | tf_op jit(solution)/shard_map/all_to_all | solution.py:477
  48.1 19.6 %all_to_all.146.refs_0_ = f32[8,4,32,256]{3,2,1,0:T(8,128)} all-to-all(f32[8,4,32,256]{3,2,1,0:T(8,128)} %shard_map.169._), channel_id=1, replica_groups=mesh['limb'=4,'coef'=8] {'coef'}, dimensions={0} | all-to-all | bytes 2097152 | tf_op jit(solution)/shard_map/all_to_all | solution.py:477
  70.4 19.6 %all_to_all.147 = f32[8,4,32,256]{3,2,1,0:T(8,128)} all-to-all(f32[8,4,32,256]{3,2,1,0:T(8,128)} %shard_map.170._), channel_id=1, replica_groups=mesh['limb'=4,'coef'=8] {'coef'}, dimensions={0} | all-to-all | bytes 2097152 | tf_op jit(solution)/shard_map/all_to_all | solution.py:477
  93.0 19.7 %all_to_all.148.refs_0_ = f32[8,4,32,256]{3,2,1,0:T(8,128)} all-to-all(f32[8,4,32,256]{3,2,1,0:T(8,128)} %shard_map.171._), channel_id=1, replica_groups=mesh['limb'=4,'coef'=8] {'coef'}, dimensions={0} | all-to-all | bytes 2097152 | tf_op jit(solution)/shard_map/all_to_all | solution.py:477
  115.4 19.5 %all_to_all.149 = f32[8,4,32,256]{3,2,1,0:T(8,128)} all-to-all(f32[8,4,32,256]{3,2,1,0:T(8,128)} %shard_map.172._), channel_id=1, replica_groups=mesh['limb'=4,'coef'=8] {'coef'}, dimensions={0} | all-to-all | bytes 2097152 | tf_op jit(solution)/shard_map/all_to_all | solution.py:477
  154.7 8.1 shard_map.173
  169.3 6.7 all-to-all-done.5.refs_0_
  182.8 12.9 %all-to-all-done.6.refs_0_ = f32[8,4,32,256]{3,2,1,0:T(8,128)S(1)} async-done(((f32[8,4,32,256]{3,2,1,0:T(8,128)}), f32[8,4,32,256]{3,2,1,0:T(8,128)S(1)}, u32[]{:S(2)}, u32[]{:S(2)}) %all-to-all-start.6) | async-done | bytes 1048608 | tf_op jit(solution)/shard_map/all_to_all | solution.py:477
  199.4 19.6 %all_to_all.150 = f32[8,4,32,256]{3,2,1,0:T(8,128)} all-to-all(f32[8,4,32,256]{3,2,1,0:T(8,128)} %shard_map.176._), channel_id=1, replica_groups=mesh['limb'=4,'coef'=8] {'coef'}, dimensions={0} | all-to-all | bytes 2097152 | tf_op jit(solution)/shard_map/all_to_all | solution.py:477
  222.5 13.7 %shard_map.177 = (f32[8,4,32,256]{3,2,1,0:T(8,128)}, f32[4,2,8,8192]{3,2,1,0:T(8,128)}) custom-call(f32[8,4,32,256]{3,2,1,0:T(8,128)} %shard_map.176._, f32[2,12,16]{2,1,0:T(8,128)} %bitcast.42, f32[32,4,32,256]{3,2,1,0:T(8,128)} %all-gather.10.cloned.1.call-done.refs_1_, f32[12,32,256]{2,1,0:T(8,128)} %reshape.27.refs_2_, ...), custom_call_target="tpu_custom_call" | custom-call | flops 16000000 | tf_op jit(solution)/shard_map/pallas_call | solution.py:506
  248.2 8.1 all-to-all-done.8.refs_0_
  270.4 5.6 all-to-all-done.10.refs_0_
  278.7 19.6 %all_to_all.151 = f32[8,4,32,256]{3,2,1,0:T(8,128)} all-to-all(f32[8,4,32,256]{3,2,1,0:T(8,128)} %shard_map.181._), channel_id=1, replica_groups=mesh['limb'=4,'coef'=8] {'coef'}, dimensions={0} | all-to-all | bytes 2097152 | tf_op jit(solution)/shard_map/all_to_all | solution.py:477
  298.2 18.8 %all_to_all.152.refs_1_ = f32[8,4,32,256]{3,2,1,0:T(8,128)S(1)} all-to-all(f32[8,4,32,256]{3,2,1,0:T(8,128)} %shard_map.179._), channel_id=1, replica_groups=mesh['limb'=4,'coef'=8] {'coef'}, dimensions={0} | all-to-all | bytes 2097152 | tf_op jit(solution)/shard_map/all_to_all | solution.py:477
  317.0 71.9 %collective-permute-start.4 = (f32[8,4,32,256]{3,2,1,0:T(8,128)S(1)}, f32[8,4,32,256]{3,2,1,0:T(8,128)}, u32[]{:S(2)}, u32[]{:S(2)}) collective-permute-start(f32[8,4,32,256]{3,2,1,0:T(8,128)S(1)} %all_to_all.152.refs_1_), channel_id=1, source_target_pairs={{0,8},{24,16},{1,9},{25,17},{2,10},{26,18},{3,11},{27,19},{4,12},{... | collective-permute-start | bytes 3145736 | tf_op jit(solution)/shard_map/ppermute | solution.py:480
  389.0 13.7 %shard_map.182 = (f32[8,4,32,256]{3,2,1,0:T(8,128)}, f32[4,2,8,8192]{3,2,1,0:T(8,128)}) custom-call(f32[8,4,32,256]{3,2,1,0:T(8,128)} %shard_map.181._, f32[2,12,16]{2,1,0:T(8,128)} %bitcast.43, f32[32,4,32,256]{3,2,1,0:T(8,128)} %all-gather.12.cloned.1.call-done.refs_1_, f32[12,32,256]{2,1,0:T(8,128)} %reshape.27.refs_2_, ...), custom_call_target="tpu_custom_call" | custom-call | flops 16000000 | tf_op jit(solution)/shard_map/pallas_call | solution.py:506
  408.6 24.9 %collective-permute-done.4.refs_2_ = f32[8,4,32,256]{3,2,1,0:T(8,128)} collective-permute-done((f32[8,4,32,256]{3,2,1,0:T(8,128)S(1)}, f32[8,4,32,256]{3,2,1,0:T(8,128)}, u32[]{:S(2)}, u32[]{:S(2)}) %collective-permute-start.4) | collective-permute-done | bytes 1048608 | tf_op jit(solution)/shard_map/ppermute | solution.py:480
  450.0 7.7 all-to-all-done.14.refs_0_
  460.5 19.5 %all_to_all.153 = f32[8,4,32,256]{3,2,1,0:T(8,128)} all-to-all(f32[8,4,32,256]{3,2,1,0:T(8,128)} %shard_map.186._), channel_id=1, replica_groups=mesh['limb'=4,'coef'=8] {'coef'}, dimensions={0} | all-to-all | bytes 2097152 | tf_op jit(solution)/shard_map/all_to_all | solution.py:477
  483.6 13.7 %shard_map.187 = (f32[8,4,32,256]{3,2,1,0:T(8,128)}, f32[4,2,8,8192]{3,2,1,0:T(8,128)}) custom-call(f32[8,4,32,256]{3,2,1,0:T(8,128)} %shard_map.186._, f32[2,12,16]{2,1,0:T(8,128)} %bitcast.44, f32[32,4,32,256]{3,2,1,0:T(8,128)} %all-gather.14.cloned.1.call-done.refs_1_, f32[12,32,256]{2,1,0:T(8,128)} %reshape.27.refs_2_, ...), custom_call_target="tpu_custom_call" | custom-call | flops 16000000 | tf_op jit(solution)/shard_map/pallas_call | solution.py:506
  503.2 42.1 %collective-permute-start.8 = (f32[8,4,32,256]{3,2,1,0:T(8,128)S(1)}, f32[8,4,32,256]{3,2,1,0:T(8,128)}, u32[]{:S(2)}, u32[]{:S(2)}) collective-permute-start(f32[8,4,32,256]{3,2,1,0:T(8,128)S(1)} %all-to-all-done.17.refs_1_), channel_id=1, source_target_pairs={{0,8},{24,16},{1,9},{25,17},{2,10},{26,18},{3,11},{27,19},{4,12},{... | collective-permute-start | bytes 3145736 | tf_op jit(solution)/shard_map/ppermute | solution.py:480
  557.7 32.4 %collective-permute-done.8.refs_2_ = f32[8,4,32,256]{3,2,1,0:T(8,128)} collective-permute-done((f32[8,4,32,256]{3,2,1,0:T(8,128)S(1)}, f32[8,4,32,256]{3,2,1,0:T(8,128)}, u32[]{:S(2)}, u32[]{:S(2)}) %collective-permute-start.8) | collective-permute-done | bytes 1048608 | tf_op jit(solution)/shard_map/ppermute | solution.py:480
  593.1 7.4 collective-permute-start.12
  608.2 7.9 collective-permute-done.6.refs_5_
  616.1 5.7 shard_map.190
  629.1 13.7 %shard_map.193 = (f32[8,4,32,256]{3,2,1,0:T(8,128)}, f32[4,2,8,8192]{3,2,1,0:T(8,128)}) custom-call(f32[8,2,32,256]{3,2,1,0:T(8,128)} %shard_map.192._, f32[2,12,16]{2,1,0:T(8,128)} %bitcast.45, f32[32,4,32,256]{3,2,1,0:T(8,128)} %all-gather.16.cloned.1.call-done.refs_1_, f32[12,32,256]{2,1,0:T(8,128)} %reshape.27.refs_2_, ...), custom_call_target="tpu_custom_call" | custom-call | flops 16000000 | tf_op jit(solution)/shard_map/pallas_call | solution.py:506
  648.0 13.9 %all-to-all-done.20.refs_0_ = f32[8,4,32,256]{3,2,1,0:T(8,128)S(1)} async-done(((f32[8,4,32,256]{3,2,1,0:T(8,128)}), f32[8,4,32,256]{3,2,1,0:T(8,128)S(1)}, u32[]{:S(2)}, u32[]{:S(2)}) %all-to-all-start.20) | async-done | bytes 1048608 | tf_op jit(solution)/shard_map/all_to_all | solution.py:477
  668.8 9.2 shard_map.195
  684.2 13.7 %shard_map.197 = (f32[8,4,32,256]{3,2,1,0:T(8,128)}, f32[4,2,8,8192]{3,2,1,0:T(8,128)}) custom-call(f32[16,4,32,256]{3,2,1,0:T(8,128)} %shard_map.196._, f32[2,12,16]{2,1,0:T(8,128)} %bitcast.46, f32[32,4,32,256]{3,2,1,0:T(8,128)} %all-gather.18.cloned.1.call-done.refs_1_, f32[12,32,256]{2,1,0:T(8,128)} %reshape.27.refs_2_, ...), custom_call_target="tpu_custom_call" | custom-call | flops 16000000 | tf_op jit(solution)/shard_map/pallas_call | solution.py:506
  697.8 19.6 %all_to_all.154.refs_0_ = f32[8,4,32,256]{3,2,1,0:T(8,128)} all-to-all(f32[8,4,32,256]{3,2,1,0:T(8,128)} %get-tuple-element.47._), channel_id=1, replica_groups=mesh['limb'=4,'coef'=8] {'coef'}, dimensions={0} | all-to-all | bytes 2097152 | tf_op jit(solution)/shard_map/all_to_all | solution.py:477
  724.5 11.8 %all-to-all-done.24.refs_1_ = f32[8,4,32,256]{3,2,1,0:T(8,128)S(1)} async-done(((f32[8,4,32,256]{3,2,1,0:T(8,128)}), f32[8,4,32,256]{3,2,1,0:T(8,128)S(1)}, u32[]{:S(2)}, u32[]{:S(2)}) %all-to-all-start.24) | async-done | bytes 1048608 | tf_op jit(solution)/shard_map/all_to_all | solution.py:477
  741.2 43.1 %collective-permute-start.16 = (f32[8,4,32,256]{3,2,1,0:T(8,128)S(1)}, f32[8,4,32,256]{3,2,1,0:T(8,128)}, u32[]{:S(2)}, u32[]{:S(2)}) collective-permute-start(f32[8,4,32,256]{3,2,1,0:T(8,128)S(1)} %all-to-all-done.24.refs_1_), channel_id=1, source_target_pairs={{0,8},{24,16},{1,9},{25,17},{2,10},{26,18},{3,11},{27,19},{4,12},{... | collective-permute-start | bytes 3145736 | tf_op jit(solution)/shard_map/ppermute | solution.py:480
  784.3 12.7 %collective-permute-start.19 = (f32[8,4,32,256]{3,2,1,0:T(8,128)S(1)}, f32[8,4,32,256]{3,2,1,0:T(8,128)}, u32[]{:S(2)}, u32[]{:S(2)}) collective-permute-start(f32[8,4,32,256]{3,2,1,0:T(8,128)S(1)} %all-to-all-done.26.refs_1_), channel_id=1, source_target_pairs={{0,8},{24,16},{1,9},{25,17},{2,10},{26,18},{3,11},{27,19},{4,12},{... | collective-permute-start | bytes 3145736 | tf_op jit(solution)/shard_map/ppermute | solution.py:480
  798.7 26.5 %collective-permute-done.16.refs_2_ = f32[8,4,32,256]{3,2,1,0:T(8,128)} collective-permute-done((f32[8,4,32,256]{3,2,1,0:T(8,128)S(1)}, f32[8,4,32,256]{3,2,1,0:T(8,128)}, u32[]{:S(2)}, u32[]{:S(2)}) %collective-permute-start.16) | collective-permute-done | bytes 1048608 | tf_op jit(solution)/shard_map/ppermute | solution.py:480
  827.5 20.0 %collective-permute-done.19.refs_2_ = f32[8,4,32,256]{3,2,1,0:T(8,128)} collective-permute-done((f32[8,4,32,256]{3,2,1,0:T(8,128)S(1)}, f32[8,4,32,256]{3,2,1,0:T(8,128)}, u32[]{:S(2)}, u32[]{:S(2)}) %collective-permute-start.19) | collective-permute-done | bytes 1048608 | tf_op jit(solution)/shard_map/ppermute | solution.py:480
  850.8 9.2 shard_map.199
  866.3 8.1 shard_map.201
  895.6 8.1 all-to-all-done.28.refs_1_
  903.8 20.1 %collective-permute-start.24 = (f32[8,2,32,256]{3,2,1,0:T(8,128)S(1)}, f32[8,2,32,256]{3,2,1,0:T(8,128)}, u32[]{:S(2)}, u32[]{:S(2)}) collective-permute-start(f32[8,2,32,256]{3,2,1,0:T(8,128)S(1)} %all-to-all-done.28.refs_1_), channel_id=1, source_target_pairs={{0,8},{24,16},{1,9},{25,17},{2,10},{26,18},{3,11},{27,19},{4,12},{... | collective-permute-start | bytes 1572872 | tf_op jit(solution)/shard_map/ppermute | solution.py:480
  924.5 7.4 collective-permute-done.24.refs_2_
  932.7 9.2 shard_map.204
  941.8 5.6 collective-permute-done.22.refs_5_
  947.5 9.2 shard_map.205
  961.9 30.6 %collective-permute-done.26.refs_5_ = f32[16,4,32,256]{3,2,1,0:T(8,128)} collective-permute-done((f32[16,4,32,256]{3,2,1,0:T(8,128)S(1)}, f32[16,4,32,256]{3,2,1,0:T(8,128)}, u32[]{:S(2)}, u32[]{:S(2)}) %collective-permute-start.26) | collective-permute-done | bytes 2097184 | tf_op jit(solution)/shard_map/ppermute | solution.py:486
  992.4 9.2 shard_map.207
  1001.6 12.2 %collective-permute-done.27.refs_5_ = f32[16,2,32,256]{3,2,1,0:T(8,128)S(1)} collective-permute-done((f32[16,2,32,256]{3,2,1,0:T(8,128)}, f32[16,2,32,256]{3,2,1,0:T(8,128)S(1)}, u32[]{:S(2)}, u32[]{:S(2)}) %collective-permute-start.27) | collective-permute-done | bytes 1048608 | tf_op jit(solution)/shard_map/ppermute | solution.py:486
  1014.8 5.8 shard_map.208
  (208 shorter events, 233.2 us)
Async XLA Ops:
  13.2 14.9 %all-to-all-start = ((f32[8,2,32,256]{3,2,1,0:T(8,128)}), f32[8,2,32,256]{3,2,1,0:T(8,128)S(1)}, u32[]{:S(2)}, u32[]{:S(2)}) async-start(f32[8,2,32,256]{3,2,1,0:T(8,128)} %shard_map.167._), calls=%async_computation | async-start | bytes 1048576 | tf_op jit(solution)/shard_map/all_to_all | solution.py:477
  18.4 136.3 %all-gather.8.cloned.1.call-start = ((), (), s32[]{:S(2)}) async-start(), calls=%async_computation.29 | async-start | bytes 2621440 | tf_op jit(solution)/shard_map/all_gather | solution.py:530
  45.1 177.4 %all-gather.10.cloned.1.call-start = ((), (), s32[]{:S(2)}) async-start(), calls=%async_computation.30 | async-start | bytes 5242880 | tf_op jit(solution)/shard_map/all_gather | solution.py:530
  90.0 299.0 %all-gather.12.cloned.1.call-start = ((), (), s32[]{:S(2)}) async-start(), calls=%async_computation.31 | async-start | bytes 5242880 | tf_op jit(solution)/shard_map/all_gather | solution.py:530
  176.8 18.9 %all-to-all-start.6 = ((f32[8,4,32,256]{3,2,1,0:T(8,128)}), f32[8,4,32,256]{3,2,1,0:T(8,128)S(1)}, u32[]{:S(2)}, u32[]{:S(2)}) async-start(f32[8,4,32,256]{3,2,1,0:T(8,128)} %shard_map.174._), calls=%async_computation.6 | async-start | bytes 2097152 | tf_op jit(solution)/shard_map/all_to_all | solution.py:477
  180.4 303.3 %all-gather.14.cloned.1.call-start = ((), (), s32[]{:S(2)}) async-start(), calls=%async_computation.32 | async-start | bytes 5242880 | tf_op jit(solution)/shard_map/all_gather | solution.py:530
  218.9 17.2 %all-to-all-start.9 = ((f32[8,2,32,256]{3,2,1,0:T(8,128)}), f32[8,2,32,256]{3,2,1,0:T(8,128)S(1)}, u32[]{:S(2)}, u32[]{:S(2)}) async-start(f32[8,2,32,256]{3,2,1,0:T(8,128)} %shard_map.175._), calls=%async_computation.9 | async-start | bytes 1048576 | tf_op jit(solution)/shard_map/all_to_all | solution.py:477
  236.2 20.1 %all-to-all-start.8 = ((f32[8,4,32,256]{3,2,1,0:T(8,128)}), f32[8,4,32,256]{3,2,1,0:T(8,128)}, u32[]{:S(2)}, u32[]{:S(2)}) async-start(f32[8,4,32,256]{3,2,1,0:T(8,128)} %get-tuple-element.37._), calls=%async_computation.8 | async-start | bytes 2097152 | tf_op jit(solution)/shard_map/all_to_all | solution.py:477
  240.9 20.4 %collective-permute-start.1 = (f32[8,2,32,256]{3,2,1,0:T(8,128)S(1)}, f32[8,2,32,256]{3,2,1,0:T(8,128)}, u32[]{:S(2)}, u32[]{:S(2)}) collective-permute-start(f32[8,2,32,256]{3,2,1,0:T(8,128)S(1)} %all-to-all-done.9.refs_1_), channel_id=1, source_target_pairs={{0,8},{24,16},{1,9},{25,17},{2,10},{26,18},{3,11},{27,19},{4,12},{... | collective-permute-start | bytes 1572872 | tf_op jit(solution)/shard_map/ppermute | solution.py:480
  256.3 19.6 %all-to-all-start.10 = ((f32[8,4,32,256]{3,2,1,0:T(8,128)}), f32[8,4,32,256]{3,2,1,0:T(8,128)}, u32[]{:S(2)}, u32[]{:S(2)}) async-start(f32[8,4,32,256]{3,2,1,0:T(8,128)} %shard_map.178._), calls=%async_computation.10 | async-start | bytes 2097152 | tf_op jit(solution)/shard_map/all_to_all | solution.py:477
  260.6 368.5 %all-gather.16.cloned.1.call-start = ((), (), s32[]{:S(2)}) async-start(), calls=%async_computation.33 | async-start | bytes 5242880 | tf_op jit(solution)/shard_map/all_gather | solution.py:530
  317.0 116.5 %collective-permute-start.4 = (f32[8,4,32,256]{3,2,1,0:T(8,128)S(1)}, f32[8,4,32,256]{3,2,1,0:T(8,128)}, u32[]{:S(2)}, u32[]{:S(2)}) collective-permute-start(f32[8,4,32,256]{3,2,1,0:T(8,128)S(1)} %all_to_all.152.refs_1_), channel_id=1, source_target_pairs={{0,8},{24,16},{1,9},{25,17},{2,10},{26,18},{3,11},{27,19},{4,12},{... | collective-permute-start | bytes 3145736 | tf_op jit(solution)/shard_map/ppermute | solution.py:480
  402.7 35.5 %all-to-all-start.12 = ((f32[8,4,32,256]{3,2,1,0:T(8,128)}), f32[8,4,32,256]{3,2,1,0:T(8,128)}, u32[]{:S(2)}, u32[]{:S(2)}) async-start(f32[8,4,32,256]{3,2,1,0:T(8,128)} %get-tuple-element.38._), calls=%async_computation.12 | async-start | bytes 2097152 | tf_op jit(solution)/shard_map/all_to_all | solution.py:477
  406.9 38.2 %collective-permute-start.3 = (f32[8,4,32,256]{3,2,1,0:T(8,128)S(1)}, f32[8,4,32,256]{3,2,1,0:T(8,128)}, u32[]{:S(2)}, u32[]{:S(2)}) collective-permute-start(f32[8,4,32,256]{3,2,1,0:T(8,128)S(1)} %all_to_all.152.refs_1_), channel_id=1, source_target_pairs={{8,16},{16,8},{9,17},{17,9},{10,18},{18,10},{11,19},{19,11},{12,20... | collective-permute-start | bytes 3145736 | tf_op jit(solution)/shard_map/ppermute | solution.py:483
  438.1 19.6 %all-to-all-start.14 = ((f32[8,4,32,256]{3,2,1,0:T(8,128)}), f32[8,4,32,256]{3,2,1,0:T(8,128)}, u32[]{:S(2)}, u32[]{:S(2)}) async-start(f32[8,4,32,256]{3,2,1,0:T(8,128)} %shard_map.183._), calls=%async_computation.14 | async-start | bytes 2097152 | tf_op jit(solution)/shard_map/all_to_all | solution.py:477
  442.4 241.8 %all-gather.18.cloned.1.call-start = ((), (), s32[]{:S(2)}) async-start(), calls=%async_computation.34 | async-start | bytes 5242880 | tf_op jit(solution)/shard_map/all_gather | solution.py:530
  480.0 18.9 %all-to-all-start.17 = ((f32[8,4,32,256]{3,2,1,0:T(8,128)}), f32[8,4,32,256]{3,2,1,0:T(8,128)S(1)}, u32[]{:S(2)}, u32[]{:S(2)}) async-start(f32[8,4,32,256]{3,2,1,0:T(8,128)} %shard_map.184._), calls=%async_computation.17 | async-start | bytes 2097152 | tf_op jit(solution)/shard_map/all_to_all | solution.py:477
  498.9 48.8 %all-to-all-start.16 = ((f32[8,4,32,256]{3,2,1,0:T(8,128)}), f32[8,4,32,256]{3,2,1,0:T(8,128)}, u32[]{:S(2)}, u32[]{:S(2)}) async-start(f32[8,4,32,256]{3,2,1,0:T(8,128)} %get-tuple-element.39._), calls=%async_computation.16 | async-start | bytes 2097152 | tf_op jit(solution)/shard_map/all_to_all | solution.py:477
  503.2 87.0 %collective-permute-start.8 = (f32[8,4,32,256]{3,2,1,0:T(8,128)S(1)}, f32[8,4,32,256]{3,2,1,0:T(8,128)}, u32[]{:S(2)}, u32[]{:S(2)}) collective-permute-start(f32[8,4,32,256]{3,2,1,0:T(8,128)S(1)} %all-to-all-done.17.refs_1_), channel_id=1, source_target_pairs={{0,8},{24,16},{1,9},{25,17},{2,10},{26,18},{3,11},{27,19},{4,12},{... | collective-permute-start | bytes 3145736 | tf_op jit(solution)/shard_map/ppermute | solution.py:480
  550.5 42.6 %all-to-all-start.21 = ((f32[8,4,32,256]{3,2,1,0:T(8,128)}), f32[8,4,32,256]{3,2,1,0:T(8,128)}, u32[]{:S(2)}, u32[]{:S(2)}) async-start(f32[8,4,32,256]{3,2,1,0:T(8,128)} %shard_map.189._), calls=%async_computation.21 | async-start | bytes 2097152 | tf_op jit(solution)/shard_map/all_to_all | solution.py:477
  554.7 61.4 %collective-permute-start.6 = (f32[16,2,32,256]{3,2,1,0:T(8,128)}, f32[16,2,32,256]{3,2,1,0:T(8,128)}, u32[]{:S(2)}, u32[]{:S(2)}) collective-permute-start(f32[16,2,32,256]{3,2,1,0:T(8,128)} %shard_map.180._), channel_id=1, source_target_pairs={{8,0},{16,24},{9,1},{17,25},{10,2},{18,26},{11,3},{19,27},{12,4},{... | collective-permute-start | bytes 3145736 | tf_op jit(solution)/shard_map/ppermute | solution.py:486
  556.0 65.8 %collective-permute-start.7 = (f32[8,4,32,256]{3,2,1,0:T(8,128)S(1)}, f32[8,4,32,256]{3,2,1,0:T(8,128)}, u32[]{:S(2)}, u32[]{:S(2)}) collective-permute-start(f32[8,4,32,256]{3,2,1,0:T(8,128)S(1)} %all-to-all-done.17.refs_1_), channel_id=1, source_target_pairs={{8,16},{16,8},{9,17},{17,9},{10,18},{18,10},{11,19},{19,11},{12,20... | collective-permute-start | bytes 3145736 | tf_op jit(solution)/shard_map/ppermute | solution.py:483
  590.1 31.7 %collective-permute-start.9 = (f32[8,4,32,256]{3,2,1,0:T(8,128)}, f32[8,4,32,256]{3,2,1,0:T(8,128)}, u32[]{:S(2)}, u32[]{:S(2)}) collective-permute-start(f32[8,4,32,256]{3,2,1,0:T(8,128)} %collective-permute-done.8.refs_2_), channel_id=1, source_target_pairs={{8,16},{16,8},{9,17},{17,9},{10,18},{18,10},{11,19},{19,11},{12,20... | collective-permute-start | bytes 3145736 | tf_op jit(solution)/shard_map/ppermute | solution.py:483
  591.8 77.0 %collective-permute-start.10 = (f32[16,4,32,256]{3,2,1,0:T(8,128)}, f32[16,4,32,256]{3,2,1,0:T(8,128)}, u32[]{:S(2)}, u32[]{:S(2)}) collective-permute-start(f32[16,4,32,256]{3,2,1,0:T(8,128)} %shard_map.185._), channel_id=1, source_target_pairs={{8,0},{16,24},{9,1},{17,25},{10,2},{18,26},{11,3},{19,27},{12,4},{... | collective-permute-start | bytes 6291464 | tf_op jit(solution)/shard_map/ppermute | solution.py:486
  593.1 54.2 %collective-permute-start.12 = (f32[8,4,32,256]{3,2,1,0:T(8,128)}, f32[8,4,32,256]{3,2,1,0:T(8,128)}, u32[]{:S(2)}, u32[]{:S(2)}) collective-permute-start(f32[8,4,32,256]{3,2,1,0:T(8,128)} %all-to-all-done.21.refs_1_), channel_id=1, source_target_pairs={{0,8},{24,16},{1,9},{25,17},{2,10},{26,18},{3,11},{27,19},{4,12},{... | collective-permute-start | bytes 3145736 | tf_op jit(solution)/shard_map/ppermute | solution.py:480
  601.5 25.3 %all-to-all-start.18 = ((f32[8,2,32,256]{3,2,1,0:T(8,128)}), f32[8,2,32,256]{3,2,1,0:T(8,128)}, u32[]{:S(2)}, u32[]{:S(2)}) async-start(f32[8,2,32,256]{3,2,1,0:T(8,128)} %shard_map.188._), calls=%async_computation.18 | async-start | bytes 1048576 | tf_op jit(solution)/shard_map/all_to_all | solution.py:477
  642.8 19.1 %all-to-all-start.20 = ((f32[8,4,32,256]{3,2,1,0:T(8,128)}), f32[8,4,32,256]{3,2,1,0:T(8,128)S(1)}, u32[]{:S(2)}, u32[]{:S(2)}) async-start(f32[8,4,32,256]{3,2,1,0:T(8,128)} %get-tuple-element.42._), calls=%async_computation.20 | async-start | bytes 2097152 | tf_op jit(solution)/shard_map/all_to_all | solution.py:477
  646.5 31.4 %collective-permute-start.11 = (f32[8,4,32,256]{3,2,1,0:T(8,128)}, f32[8,4,32,256]{3,2,1,0:T(8,128)S(1)}, u32[]{:S(2)}, u32[]{:S(2)}) collective-permute-start(f32[8,4,32,256]{3,2,1,0:T(8,128)} %all-to-all-done.21.refs_1_), channel_id=1, source_target_pairs={{8,16},{16,8},{9,17},{17,9},{10,18},{18,10},{11,19},{19,11},{12,20... | collective-permute-start | bytes 3145736 | tf_op jit(solution)/shard_map/ppermute | solution.py:483
  647.2 30.7 %collective-permute-start.13 = (f32[8,4,32,256]{3,2,1,0:T(8,128)}, f32[8,4,32,256]{3,2,1,0:T(8,128)S(1)}, u32[]{:S(2)}, u32[]{:S(2)}) collective-permute-start(f32[8,4,32,256]{3,2,1,0:T(8,128)} %collective-permute-done.12.refs_2_), channel_id=1, source_target_pairs={{8,16},{16,8},{9,17},{17,9},{10,18},{18,10},{11,19},{19,11},{12,20... | collective-permute-start | bytes 3145736 | tf_op jit(solution)/shard_map/ppermute | solution.py:483
  661.9 35.9 %all-to-all-start.25 = ((f32[8,2,32,256]{3,2,1,0:T(8,128)}), f32[8,2,32,256]{3,2,1,0:T(8,128)}, u32[]{:S(2)}, u32[]{:S(2)}) async-start(f32[8,2,32,256]{3,2,1,0:T(8,128)} %shard_map.192._), calls=%async_computation.25 | async-start | bytes 1048576 | tf_op jit(solution)/shard_map/all_to_all | solution.py:477
  717.4 18.9 %all-to-all-start.24 = ((f32[8,4,32,256]{3,2,1,0:T(8,128)}), f32[8,4,32,256]{3,2,1,0:T(8,128)S(1)}, u32[]{:S(2)}, u32[]{:S(2)}) async-start(f32[8,4,32,256]{3,2,1,0:T(8,128)} %shard_map.194._), calls=%async_computation.24 | async-start | bytes 2097152 | tf_op jit(solution)/shard_map/all_to_all | solution.py:477
  721.0 145.3 %all-gather.20.cloned.1.call-start = ((), (), s32[]{:S(2)}) async-start(), calls=%async_computation.35 | async-start | bytes 2621440 | tf_op jit(solution)/shard_map/all_gather | solution.py:530
  736.3 48.0 %all-to-all-start.26 = ((f32[8,4,32,256]{3,2,1,0:T(8,128)}), f32[8,4,32,256]{3,2,1,0:T(8,128)S(1)}, u32[]{:S(2)}, u32[]{:S(2)}) async-start(f32[8,4,32,256]{3,2,1,0:T(8,128)} %shard_map.198._), calls=%async_computation.26 | async-start | bytes 2097152 | tf_op jit(solution)/shard_map/all_to_all | solution.py:477
  739.9 109.7 %collective-permute-start.14 = (f32[16,4,32,256]{3,2,1,0:T(8,128)}, f32[16,4,32,256]{3,2,1,0:T(8,128)}, u32[]{:S(2)}, u32[]{:S(2)}) collective-permute-start(f32[16,4,32,256]{3,2,1,0:T(8,128)} %shard_map.191._), channel_id=1, source_target_pairs={{8,0},{16,24},{9,1},{17,25},{10,2},{18,26},{11,3},{19,27},{12,4},{... | collective-permute-start | bytes 6291464 | tf_op jit(solution)/shard_map/ppermute | solution.py:486
  741.2 84.0 %collective-permute-start.16 = (f32[8,4,32,256]{3,2,1,0:T(8,128)S(1)}, f32[8,4,32,256]{3,2,1,0:T(8,128)}, u32[]{:S(2)}, u32[]{:S(2)}) collective-permute-start(f32[8,4,32,256]{3,2,1,0:T(8,128)S(1)} %all-to-all-done.24.refs_1_), channel_id=1, source_target_pairs={{0,8},{24,16},{1,9},{25,17},{2,10},{26,18},{3,11},{27,19},{4,12},{... | collective-permute-start | bytes 3145736 | tf_op jit(solution)/shard_map/ppermute | solution.py:480
  784.3 63.2 %collective-permute-start.19 = (f32[8,4,32,256]{3,2,1,0:T(8,128)S(1)}, f32[8,4,32,256]{3,2,1,0:T(8,128)}, u32[]{:S(2)}, u32[]{:S(2)}) collective-permute-start(f32[8,4,32,256]{3,2,1,0:T(8,128)S(1)} %all-to-all-done.26.refs_1_), channel_id=1, source_target_pairs={{0,8},{24,16},{1,9},{25,17},{2,10},{26,18},{3,11},{27,19},{4,12},{... | collective-permute-start | bytes 3145736 | tf_op jit(solution)/shard_map/ppermute | solution.py:480
  797.0 63.0 %collective-permute-start.15 = (f32[8,4,32,256]{3,2,1,0:T(8,128)S(1)}, f32[8,4,32,256]{3,2,1,0:T(8,128)}, u32[]{:S(2)}, u32[]{:S(2)}) collective-permute-start(f32[8,4,32,256]{3,2,1,0:T(8,128)S(1)} %all-to-all-done.24.refs_1_), channel_id=1, source_target_pairs={{8,16},{16,8},{9,17},{17,9},{10,18},{18,10},{11,19},{19,11},{12,20... | collective-permute-start | bytes 3145736 | tf_op jit(solution)/shard_map/ppermute | solution.py:483
  825.2 34.9 %collective-permute-start.17 = (f32[8,4,32,256]{3,2,1,0:T(8,128)}, f32[8,4,32,256]{3,2,1,0:T(8,128)}, u32[]{:S(2)}, u32[]{:S(2)}) collective-permute-start(f32[8,4,32,256]{3,2,1,0:T(8,128)} %collective-permute-done.16.refs_2_), channel_id=1, source_target_pairs={{8,16},{16,8},{9,17},{17,9},{10,18},{18,10},{11,19},{19,11},{12,20... | collective-permute-start | bytes 3145736 | tf_op jit(solution)/shard_map/ppermute | solution.py:483
  826.8 51.8 %collective-permute-start.18 = (f32[8,4,32,256]{3,2,1,0:T(8,128)S(1)}, f32[8,4,32,256]{3,2,1,0:T(8,128)S(1)}, u32[]{:S(2)}, u32[]{:S(2)}) collective-permute-start(f32[8,4,32,256]{3,2,1,0:T(8,128)S(1)} %all-to-all-done.26.refs_1_), channel_id=1, source_target_pairs={{8,16},{16,8},{9,17},{17,9},{10,18},{18,10},{11,19},{19,11},{12,20... | collective-permute-start | bytes 3145736 | tf_op jit(solution)/shard_map/ppermute | solution.py:483
  847.5 31.1 %collective-permute-start.20 = (f32[8,4,32,256]{3,2,1,0:T(8,128)}, f32[8,4,32,256]{3,2,1,0:T(8,128)}, u32[]{:S(2)}, u32[]{:S(2)}) collective-permute-start(f32[8,4,32,256]{3,2,1,0:T(8,128)} %collective-permute-done.19.refs_2_), channel_id=1, source_target_pairs={{8,16},{16,8},{9,17},{17,9},{10,18},{18,10},{11,19},{19,11},{12,20... | collective-permute-start | bytes 3145736 | tf_op jit(solution)/shard_map/ppermute | solution.py:483
  849.5 83.1 %collective-permute-start.21 = (f32[16,4,32,256]{3,2,1,0:T(8,128)}, f32[16,4,32,256]{3,2,1,0:T(8,128)}, u32[]{:S(2)}, u32[]{:S(2)}) collective-permute-start(f32[16,4,32,256]{3,2,1,0:T(8,128)} %shard_map.196._), channel_id=1, source_target_pairs={{8,0},{16,24},{9,1},{17,25},{10,2},{18,26},{11,3},{19,27},{12,4},{... | collective-permute-start | bytes 6291464 | tf_op jit(solution)/shard_map/ppermute | solution.py:486
  865.0 82.5 %collective-permute-start.22 = (f32[16,4,32,256]{3,2,1,0:T(8,128)}, f32[16,4,32,256]{3,2,1,0:T(8,128)}, u32[]{:S(2)}, u32[]{:S(2)}) collective-permute-start(f32[16,4,32,256]{3,2,1,0:T(8,128)} %shard_map.200._), channel_id=1, source_target_pairs={{8,0},{16,24},{9,1},{17,25},{10,2},{18,26},{11,3},{19,27},{12,4},{... | collective-permute-start | bytes 6291464 | tf_op jit(solution)/shard_map/ppermute | solution.py:486
  874.4 13.9 %all-to-all-start.27 = ((f32[8,2,32,256]{3,2,1,0:T(8,128)}), f32[8,2,32,256]{3,2,1,0:T(8,128)}, u32[]{:S(2)}, u32[]{:S(2)}) async-start(f32[8,2,32,256]{3,2,1,0:T(8,128)} %get-tuple-element.52._), calls=%async_computation.27 | async-start | bytes 1048576 | tf_op jit(solution)/shard_map/all_to_all | solution.py:477
  894.1 98.3 %collective-permute-start.26 = (f32[16,4,32,256]{3,2,1,0:T(8,128)S(1)}, f32[16,4,32,256]{3,2,1,0:T(8,128)}, u32[]{:S(2)}, u32[]{:S(2)}) collective-permute-start(f32[16,4,32,256]{3,2,1,0:T(8,128)S(1)} %copy-done.6), channel_id=1, source_target_pairs={{8,0},{16,24},{9,1},{17,25},{10,2},{18,26},{11,3},{19,27},{12,4},{... | collective-permute-start | bytes 6291464 | tf_op jit(solution)/shard_map/ppermute | solution.py:486
  903.8 28.2 %collective-permute-start.24 = (f32[8,2,32,256]{3,2,1,0:T(8,128)S(1)}, f32[8,2,32,256]{3,2,1,0:T(8,128)}, u32[]{:S(2)}, u32[]{:S(2)}) collective-permute-start(f32[8,2,32,256]{3,2,1,0:T(8,128)S(1)} %all-to-all-done.28.refs_1_), channel_id=1, source_target_pairs={{0,8},{24,16},{1,9},{25,17},{2,10},{26,18},{3,11},{27,19},{4,12},{... | collective-permute-start | bytes 1572872 | tf_op jit(solution)/shard_map/ppermute | solution.py:480
  923.8 32.8 %collective-permute-start.23 = (f32[8,2,32,256]{3,2,1,0:T(8,128)S(1)}, f32[8,2,32,256]{3,2,1,0:T(8,128)S(1)}, u32[]{:S(2)}, u32[]{:S(2)}) collective-permute-start(f32[8,2,32,256]{3,2,1,0:T(8,128)S(1)} %all-to-all-done.28.refs_1_), channel_id=1, source_target_pairs={{8,16},{16,8},{9,17},{17,9},{10,18},{18,10},{11,19},{19,11},{12,20... | collective-permute-start | bytes 1572872 | tf_op jit(solution)/shard_map/ppermute | solution.py:483
  932.0 24.7 %collective-permute-start.25 = (f32[8,2,32,256]{3,2,1,0:T(8,128)}, f32[8,2,32,256]{3,2,1,0:T(8,128)S(1)}, u32[]{:S(2)}, u32[]{:S(2)}) collective-permute-start(f32[8,2,32,256]{3,2,1,0:T(8,128)} %collective-permute-done.24.refs_2_), channel_id=1, source_target_pairs={{8,16},{16,8},{9,17},{17,9},{10,18},{18,10},{11,19},{19,11},{12,20... | collective-permute-start | bytes 1572872 | tf_op jit(solution)/shard_map/ppermute | solution.py:483
  960.6 53.2 %collective-permute-start.27 = (f32[16,2,32,256]{3,2,1,0:T(8,128)}, f32[16,2,32,256]{3,2,1,0:T(8,128)S(1)}, u32[]{:S(2)}, u32[]{:S(2)}) collective-permute-start(f32[16,2,32,256]{3,2,1,0:T(8,128)} %shard_map.206._), channel_id=1, source_target_pairs={{8,0},{16,24},{9,1},{17,25},{10,2},{18,26},{11,3},{19,27},{12,4},{... | collective-permute-start | bytes 3145736 | tf_op jit(solution)/shard_map/ppermute | solution.py:486
  (34 other events, 700.2 us)
Sparse Core Ops, SparseCore 0:
  45.2 44.9 all-gather.7
  91.8 79.5 all-gather.9
  173.0 79.2 all-gather.11
  253.7 102.9 all-gather.13
  358.1 108.7 all-gather.15
  480.2 148.4 all-gather.17
  723.4 97.8 all-gather.19
